TPU v7x, 256 devices: a whole 4x4x8 slice. The times are simulated.
256 devices in a mesh: morton: 64 (over x, z, core), grp: 4 (over y).
Axes of the slice: x: 4, y: 4, z: 8, core: 2. Of those that a mesh axis runs over, the one named last changes fastest.
Arguments:
- multipoles: float32 [16384, 152], P(('morton', 'grp')), may hold values from -6 to 6
- chebyshev: float32 [16384, 560], P(('morton', 'grp')), may hold values from -6 to 6
- ghost_rows: int32 [4096, 64], P('morton'), may hold values from 0 to 255
- far_src: int32 [16384, 189], P(('morton', 'grp')), may hold values from 0 to 4351
- far_kind: int32 [16384, 189], P(('morton', 'grp')), may hold values from 0 to 15
- far_count: int32 [16384], P(('morton', 'grp')), may hold values from 1 to 189
- near_src: int32 [16384, 27], P(('morton', 'grp')), may hold values from 0 to 1087, as said below
- near_kind: int32 [16384, 27], P(('morton', 'grp')), may hold values from 0 to 3
- far_ops: float32 [16, 152, 152], replicated, may hold values from -0.046875 to 0.046875
- near_ops: float32 [4, 560, 560], replicated, may hold values from -0.046875 to 0.046875
- local_to_target: float32 [152, 560], replicated, may hold values from -0.5 to 0.5
Outputs:
- potential: float32 [16384, 560], P(('morton', 'grp'))
Inputs may be any that keep to these rules, and one draw needn't show every extreme that they name: Entries below 256 name a box of the target's own range; the others name ghost number far_src - 256 of its far ghost list. Entries below 64 name a box of the target's own device; the others name ghost number near_src - 64 of its range's near ghost list.
All inputs are finite; a program needn't handle non-finite values.
Results may differ from a plain program's by a relative error of at most 0.0003.
Values sent between devices are 32-bit elements; how exact they have to be, the bound alone decides.
A program may use at most 64 MiB of HBM per device.

v0:
```python
import jax
import jax.numpy as jnp
from jax import lax
from jax.sharding import Mesh
from jax.sharding import PartitionSpec as P

NCAP = 16
MORTON = ("morton_0", "morton_1", "morton_2")
MORTON_GRP = ("morton_0", "morton_1", "morton_2", "grp")


def split_up(value, dim, devices):
    shape = value.shape
    tiles = value.reshape(*shape[:dim], devices, shape[dim] // devices, *shape[dim + 1 :])
    return jnp.moveaxis(tiles, dim, 0)


def joined_along(tiles, dim):
    tiles = jnp.moveaxis(tiles, 0, dim)
    shape = tiles.shape
    return tiles.reshape(*shape[:dim], shape[dim] * shape[dim + 1], *shape[dim + 2 :])


def turned_blocks(tiles, axes, order):
    shape = [lax.axis_size(a) for a in axes]
    tiles = tiles.reshape(*shape, *tiles.shape[1:])
    for k in order:
        tiles = lax.all_to_all(tiles, axes[k], split_axis=k, concat_axis=k, tiled=True)
    return tiles.reshape(-1, *tiles.shape[len(axes) :])


def core_and_chips(value, groups, order, split_dim, concat_dim):
    devices = lax.axis_size(groups[0]) * lax.axis_size(groups[1])
    tiles = split_up(value, split_dim, devices)
    return joined_along(turned_blocks(tiles, groups, order), concat_dim)


def class_sum(lookup, indices, weight, class_ids, classes):
    targets, slot_count = indices.shape
    picked = lookup[indices] * weight[:, :, None]
    segment = (jnp.arange(targets, dtype=jnp.int32)[:, None] * classes + class_ids).reshape(-1)
    summed = jax.ops.segment_sum(
        picked.reshape(targets * slot_count, lookup.shape[1]),
        segment,
        num_segments=targets * classes,
    )
    return summed.reshape(targets, classes, lookup.shape[1])


def evaluate(
    far_table,
    near_table,
    far_src,
    far_kind,
    far_count,
    near_src,
    near_kind,
    far_ops,
    near_ops,
    local_to_target,
):
    active = (jnp.arange(far_src.shape[1], dtype=jnp.int32)[None, :] < far_count[:, None]).astype(
        jnp.float32
    )
    far_sum = class_sum(far_table, far_src, active, far_kind, far_ops.shape[0])
    local_field = jnp.einsum("tkp,kpq->tq", far_sum, far_ops, precision=lax.Precision.HIGHEST)
    unit_weight = jnp.ones(near_src.shape, jnp.float32)
    near_sum = class_sum(near_table, near_src, unit_weight, near_kind, near_ops.shape[0])
    near_field = jnp.einsum("tkc,kcd->td", near_sum, near_ops, precision=lax.Precision.HIGHEST)
    return jnp.dot(local_field, local_to_target, precision=lax.Precision.HIGHEST) + near_field


def shards(
    multipoles,
    chebyshev,
    ghost_rows,
    far_src,
    far_kind,
    far_count,
    near_src,
    near_kind,
    far_ops,
    near_ops,
    local_to_target,
):
    helpers = lax.axis_size("grp")
    width_p = multipoles.shape[1]
    width_q = chebyshev.shape[1]
    range_multi, range_cheb = (
        lax.all_gather(multipoles, "grp", axis=0, tiled=True),
        lax.all_gather(chebyshev, "grp", axis=0, tiled=True),
    )
    capacity = ghost_rows.shape[1]
    near_slots = NCAP
    far_share = capacity // helpers
    near_share = near_slots // helpers
    helper = lax.axis_index("grp")
    far_chosen = lax.dynamic_slice_in_dim(ghost_rows, helper * far_share, far_share, 1)
    near_chosen = lax.dynamic_slice_in_dim(ghost_rows, helper * near_share, near_share, 1)
    ghost_multi, ghost_cheb = (
        core_and_chips(
            range_multi[far_chosen], (("morton_0", "morton_1"), "morton_2"), (1, 0), 0, 0
        ),
        core_and_chips(
            range_cheb[near_chosen], (("morton_0", "morton_1"), "morton_2"), (1, 0), 0, 0
        ),
    )
    ghost_multi, ghost_cheb = (
        lax.all_gather(ghost_multi, "grp", axis=1, tiled=True),
        lax.all_gather(ghost_cheb, "grp", axis=1, tiled=True),
    )
    far_table = jnp.concatenate([range_multi, ghost_multi.reshape(-1, width_p)], axis=0)
    near_table = jnp.concatenate([chebyshev, ghost_cheb.reshape(-1, width_q)], axis=0)
    targets = far_src.shape[0]
    block_rows = min(128, targets)
    num_blocks = targets // block_rows
    pieces = (
        far_src.reshape(num_blocks, block_rows, -1),
        far_kind.reshape(num_blocks, block_rows, -1),
        far_count.reshape(num_blocks, block_rows),
        near_src.reshape(num_blocks, block_rows, -1),
        near_kind.reshape(num_blocks, block_rows, -1),
    )

    def run_block(parts):
        return evaluate(
            far_table,
            near_table,
            parts[0],
            parts[1],
            parts[2],
            parts[3],
            parts[4],
            far_ops,
            near_ops,
            local_to_target,
        )

    result = lax.map(run_block, pieces)
    return result.reshape(targets, width_q)


def solution(mesh):
    split = Mesh(
        mesh.devices.reshape(4, 8, 2, mesh.shape["grp"]),
        ("morton_0", "morton_1", "morton_2", "grp"),
    )
    placed = (
        P(MORTON_GRP, None),
        P(MORTON_GRP, None),
        P(MORTON, None),
        P(MORTON_GRP, None),
        P(MORTON_GRP, None),
        P(MORTON_GRP),
        P(MORTON_GRP, None),
        P(MORTON_GRP, None),
        P(),
        P(),
        P(),
    )
    return jax.shard_map(
        shards, mesh=split, in_specs=placed, out_specs=P(MORTON_GRP, None), check_vma=False
    )
```

profile of v0, /device:TPU:1, one launch (start us, length us, event | category | flops | bytes accessed | tf_op | source)
XLA Modules:
  0.0 330.2 jit_solution(2836283830783867841)
XLA Ops:
  6.5 0.0 copy-start
  6.5 0.0 all-gather.5.cloned.1.call-start
  6.5 1.0 compare_select_fusion.1
  7.5 0.1 reshape.141
  7.6 13.1 %all_gather.14 = f32[256,560]{1,0:T(8,128)S(1)} all-gather(f32[64,560]{1,0:T(8,128)} %param.12), channel_id=1, replica_groups=mesh['morton_0'=4,'morton_1'=8,'morton_2'=2,'grp'=4] {'grp'}, dimensions={0}, use_global_device_ids=true | all-gather | bytes 716800 | tf_op jit(solution)/shard_map/all_gather | solution.py:91
  20.8 1.9 gather_fusion.1
  22.7 0.0 copy-start.2
  22.7 0.0 copy-start.3
  22.7 1.3 reshape_reshape.14
  24.0 0.1 copy.28
  24.1 7.9 %all_to_all.20 = f32[32,2,1,4,560]{4,3,0,2,1:T(4,128)S(1)} all-to-all(f32[32,2,1,4,560]{4,3,0,2,1:T(4,128)S(1)} %copy.28), channel_id=1, replica_groups=mesh['morton_0'=4,'morton_1'=8,'morton_2'=2,'grp'=4] {'morton_2'}, dimensions={1} | all-to-all | bytes 1146880 | tf_op jit(solution)/shard_map/all_to_all | solution.py:28
  32.0 0.1 copy.29
  32.0 25.9 %all_to_all.21 = f32[32,2,1,4,560]{4,3,1,2,0:T(4,128)S(1)} all-to-all(f32[32,2,1,4,560]{4,3,1,2,0:T(4,128)S(1)} %copy.29), channel_id=1, replica_groups=mesh['morton_0'=4,'morton_1'=8,'morton_2'=2,'grp'=4] {'morton_0','morton..., dimensions={0} | all-to-all | bytes 1146880 | tf_op jit(solution)/shard_map/all_to_all | solution.py:28
  57.9 1.0 copy.30
  58.9 0.0 all-gather.5.cloned.1.call-update
  58.9 0.0 all-gather.3.cloned.1.call-start
  58.9 0.0 copy-done.2
  58.9 0.1 compare_select_fusion.2
  59.0 0.1 reshape.125
  59.1 0.0 copy-done.3
  59.1 9.9 %all_gather.12 = f32[256,152]{1,0:T(8,128)S(1)} all-gather(f32[64,152]{1,0:T(8,128)S(1)} %copy-done.3), channel_id=1, replica_groups=mesh['morton_0'=4,'morton_1'=8,'morton_2'=2,'grp'=4] {'grp'}, dimensions={0}, use_global_device_ids=true | all-gather | bytes 194560 | tf_op jit(solution)/shard_map/all_gather | solution.py:90
  69.0 4.6 %gather_fusion = f32[1024,152]{1,0:T(8,128)} fusion(f32[256,152]{1,0:T(8,128)S(1)} %all_gather.12, s32[1024]{0:T(1024)S(1)} %broadcast_clamp_fusion), kind=kCustom, calls=%fused_computation | custom fusion | bytes 1249280 | tf_op jit(solution)/shard_map/gather | solution.py:102
  73.6 0.0 copy-start.4
  73.6 0.0 copy-start.5
  73.6 0.0 copy-start.8
  73.6 1.3 copy.24
  75.0 0.0 copy-start.6
  75.0 0.0 copy-start.7
  75.0 10.5 %all_to_all.22 = f32[32,2,1,16,152]{4,3,0,2,1:T(8,128)S(1)} all-to-all(f32[32,2,1,16,152]{4,3,0,2,1:T(8,128)S(1)} %copy.24), channel_id=1, replica_groups=mesh['morton_0'=4,'morton_1'=8,'morton_2'=2,'grp'=4] {'morton_2'}, dimensions={1} | all-to-all | bytes 1245184 | tf_op jit(solution)/shard_map/all_to_all | solution.py:28
  85.5 0.1 copy.25
  85.6 0.0 copy-start.1
  85.6 30.6 %all_to_all.23 = f32[32,2,1,16,152]{4,3,1,2,0:T(8,128)} all-to-all(f32[32,2,1,16,152]{4,3,1,2,0:T(8,128)S(1)} %copy.25), channel_id=1, replica_groups=mesh['morton_0'=4,'morton_1'=8,'morton_2'=2,'grp'=4] {'morton_0','morton..., dimensions={0} | all-to-all | bytes 1245184 | tf_op jit(solution)/shard_map/all_to_all | solution.py:28
  116.2 0.0 all-gather.3.cloned.1.call-update
  116.2 0.0 copy-done.4
  116.3 0.2 reshape.133
  116.5 0.0 copy-done.5
  116.5 0.1 broadcast_add_fusion
  116.6 0.8 reshape.157
  117.4 0.0 copy-done.8
  117.4 0.1 fusion.9
  117.5 0.8 reshape.122
  118.3 0.0 copy-done.6
  118.3 0.1 copy.32
  118.4 0.1 reshape.149
  118.5 0.0 copy-done.7
  118.6 0.1 copy.27
  118.6 0.1 reshape.165
  118.8 0.6 pad_clamp_fusion
  119.4 0.0 all-gather.5.cloned.1.call-done
  119.4 3.3 copy.31
  122.7 0.0 copy-done.1
  122.7 1.7 pad_maximum_fusion.1
  124.4 30.8 %scatter_custom_fusion.1 = f32[256,560]{1,0:T(8,128)} fusion(s32[1728]{0:T(1024)S(1)} %reshape.165, f32[1088,560]{1,0:T(8,128)} %pad_maximum_fusion.1, s32[2048]{0:T(1024)S(1)} %pad_clamp_fusion.1, f32[]{:T(128)} %constant.14.clone.1), kind=kCustom, calls=%fused_computation.10 | custom fusion | flops 967680 | bytes 573952 | tf_op jit(solution)/shard_map/while/body/eval_jaxpr/scatter-add | solution.py:42
  155.2 1.3 reshape.121
  156.5 6.8 %convolution_bitcast_fusion = f32[64,560]{1,0:T(8,128)} fusion(f32[4,560,560]{2,1,0:T(8,128)} %param.20, f32[64,4,560]{2,1,0:T(4,128)S(1)} %reshape.121), kind=kOutput, calls=%fused_computation.13 | convolution fusion | flops 963379200 | bytes 5734400 | tf_op jit(solution)/shard_map/while/body/eval_jaxpr/tkc,kcd->td/dot_general | solution.py:69
  163.3 4.0 %all-gather.3.cloned.1.call-done = f32[64,64,152]{2,1,0:T(8,128)} async-done(((f32[64,16,152]{2,1,0:T(8,128)}), f32[64,64,152]{2,1,0:T(8,128)}) %all-gather.3.cloned.1.call-update) | async-done | bytes 2490384 | tf_op jit(solution)/shard_map/all_gather | solution.py:109
  167.3 4.6 %pad_maximum_fusion = f32[4352,152]{1,0:T(8,128)} fusion(f32[4096,152]{1,0:T(8,128)} %bitcast.16, f32[256,152]{1,0:T(8,128)S(1)} %all_gather.12), kind=kLoop, calls=%fused_computation.9 | loop fusion | flops 661504 | bytes 5292032 | tf_op jit(solution)/shard_map/concatenate | solution.py:112
  171.9 147.0 %scatter_custom_fusion = f32[1024,152]{1,0:T(8,128)S(1)} fusion(s32[12096]{0:T(1024)} %reshape.157, f32[12096]{0:T(1024)} %reshape.122, f32[]{:T(128)} %constant.14.clone.1, f32[4352,152]{1,0:T(8,128)} %pad_maximum_fusion, s32[12288]{0:T(1024)} %pad_clamp_fusion), kind=kCustom, calls=%fused_computation.6 | custom fusion | flops 3677184 | bytes 5177856 | tf_op jit(solution)/shard_map/while/body/eval_jaxpr/scatter-add | solution.py:42
  318.9 0.0 copy-done
  318.9 2.3 convolution_bitcast_fusion.1
  321.3 2.1 convolution_add_fusion
  (8 shorter events, 0.0 us)
Async XLA Ops:
  6.5 312.4 %copy-start = (f32[16,152,152]{2,1,0:T(8,128)S(1)}, f32[16,152,152]{2,1,0:T(8,128)}, u32[]{:S(2)}) copy-start(f32[16,152,152]{2,1,0:T(8,128)} %param.19) | copy-start | bytes 4435972
  6.5 112.9 %all-gather.5.cloned.1.call-start = ((), (), s32[]{:S(2)}) async-start(), calls=%async_computation.5 | async-start | bytes 3276800 | tf_op jit(solution)/shard_map/all_gather | solution.py:110
  22.7 36.3 %copy-start.2 = (s32[64,64]{1,0:T(8,128)S(1)}, s32[64,64]{1,0:T(8,128)}, u32[]{:S(2)}) copy-start(s32[64,64]{1,0:T(8,128)} %param.13) | copy-start | bytes 49156
  22.7 36.4 %copy-start.3 = (f32[64,152]{1,0:T(8,128)S(1)}, f32[64,152]{1,0:T(8,128)}, u32[]{:S(2)}) copy-start(f32[64,152]{1,0:T(8,128)} %param.11) | copy-start | bytes 116740
  58.9 108.4 %all-gather.3.cloned.1.call-start = ((), (), s32[]{:S(2)}) async-start(), calls=%async_computation.4 | async-start | bytes 5242880 | tf_op jit(solution)/shard_map/all_gather | solution.py:109
  73.6 42.6 %copy-start.4 = (s32[64,189]{1,0:T(8,128)S(1)}, s32[64,189]{1,0:T(8,128)}, u32[]{:S(2)}) copy-start(s32[64,189]{1,0:T(8,128)} %param.14) | copy-start | bytes 145156
  73.6 42.9 %copy-start.5 = (s32[64,189]{1,0:T(8,128)S(1)}, s32[64,189]{1,0:T(8,128)}, u32[]{:S(2)}) copy-start(s32[64,189]{1,0:T(8,128)} %param.15) | copy-start | bytes 145156
  73.6 43.8 %copy-start.8 = (s32[64]{0:T(128)S(1)}, s32[64]{0:T(128)}, u32[]{:S(2)}) copy-start(s32[64]{0:T(128)} %param.16) | copy-start | bytes 772
  75.0 43.3 %copy-start.6 = (s32[64,27]{0,1:T(8,128)S(1)}, s32[64,27]{0,1:T(8,128)}, u32[]{:S(2)}) copy-start(s32[64,27]{0,1:T(8,128)} %param.17) | copy-start | bytes 20740
  75.0 43.5 %copy-start.7 = (s32[64,27]{0,1:T(8,128)S(1)}, s32[64,27]{0,1:T(8,128)}, u32[]{:S(2)}) copy-start(s32[64,27]{0,1:T(8,128)} %param.18) | copy-start | bytes 20740
  85.6 37.1 %copy-start.1 = (f32[64,560]{1,0:T(8,128)S(1)}, f32[64,560]{1,0:T(8,128)}, u32[]{:S(2)}) copy-start(f32[64,560]{1,0:T(8,128)} %param.12) | copy-start | bytes 430084
Sparse Core Ops, SparseCore 0:
  59.0 37.8 all-gather.4
  116.4 50.8 all-gather.2
where the time goes:
time: 332 us; the launch traced here: 330 us
  other arithmetic  186 us (56%)
  blocking collectives  97.9 us (29%)
  local copies, waits for them, and re-layouts  17.4 us (5%)
  between operations  13.6 us (4%)
  matrix products  11.2 us (3%)
  waiting for transfers between devices  4.05 us (1%)
    scatter-add x2, other arithmetic, class_sum(): jax.ops.segment_sum(picked.reshape(targets * slot_count, lookup.shape[1])...  178 us
    all_to_all x4, blocking collectives, turned_blocks(): lax.all_to_all(tiles, axes[k], split_axis=k, concat_axis=k, tiled=True)  74.9 us
    all_gather x1, blocking collectives, shards(): lax.all_gather(chebyshev, 'grp', axis=0, tiled=True)  13.1 us
    all_gather x1, blocking collectives, shards(): lax.all_gather(multipoles, 'grp', axis=0, tiled=True)  9.88 us
    dot_general x1, matrix products, evaluate(): jnp.einsum('tkc,kcd->td', near_sum, near_ops, precision=lax.Precision.HIG...  6.76 us
  transfers between devices with their start and end apart: 2, of which 1 were waited for; matrix products, arithmetic and copies ran while one was open for 16% of the time, Pallas kernels for 0%

commit v1 on v0

v1 whole, which is shorter than its diff:
```python
import functools

import jax
import jax.numpy as jnp
from jax import lax
from jax.experimental import pallas as pl
from jax.experimental.pallas import tpu as pltpu
from jax.sharding import PartitionSpec as P

MESH = pl.DeviceIdType.MESH
BF = jnp.bfloat16
F32 = jnp.float32
I32 = jnp.int32

PW = 152
TW = PW - 128
QW = 560
QP = 640
FAR = 189
NEAR = 27
NEAR_AT = 192
CAP = 64
NCAP = 16
FCLS = 16
NCLS = 4
BOX = 64
KEYS = 160
SW = 1152


def split2(x):
    hi = x.astype(BF)
    return hi, (x - hi.astype(F32)).astype(BF)


def dot(a, b):
    return jnp.dot(a, b, preferred_element_type=F32)


def iota(shape, dim):
    return lax.broadcasted_iota(I32, shape, dim)


def evaluate(
    sizes,
    multi,
    cheb,
    ghost,
    idx,
    far_ops,
    near_ops,
    to_target,
    out,
    mall,
    call,
    iall,
    send_f,
    send_n,
    recv_f,
    recv_n,
    pick_f,
    pick_n,
    pick_e,
    w_pick,
    key_l,
    key_r,
    count,
    ncount,
    w_main,
    w_tail,
    w_near,
    far_main,
    far_tail,
    ops_f,
    ops_n,
    ops_t,
    f_hi,
    f_lo,
    n_hi,
    n_lo,
    t_hi,
    t_lo,
    local_sum,
    near_sum,
    nh,
    nl,
    rs_send,
    rs_recv,
    y_send,
    y_recv,
    f_send,
    f_recv,
    n_send,
    n_recv,
    r_send,
    r_recv,
    load,
):
    xs, zs, cs = sizes
    ranges = xs * zs * cs
    me = lax.axis_index("morton")
    h = lax.axis_index("grp")
    my_x = me // (zs * cs)
    my_z = (me // cs) % zs
    my_c = me % cs

    def helper(d):
        return (me, (h + d) % 4)

    def peer(o):
        zz = o % zs
        dz = ((zz + 1) // 2) * (1 - 2 * ((zz + 1) % 2))
        dx = (o // zs) % xs
        dc = o // (zs * xs)
        x = (my_x + dx) % xs
        z = (my_z + dz + zs) % zs
        return (x * zs + z) * cs + (my_c + dc) % cs

    loads = [
        pltpu.make_async_copy(far_ops, ops_f, load.at[0]),
        pltpu.make_async_copy(near_ops, ops_n, load.at[1]),
        pltpu.make_async_copy(to_target, ops_t, load.at[2]),
    ]
    for copy in loads:
        copy.start()

    barrier = pltpu.get_barrier_semaphore()
    for d in range(1, 4):
        pl.semaphore_signal(barrier, inc=1, device_id=helper(d), device_id_type=MESH)

    def greet(o, _):
        pl.semaphore_signal(barrier, inc=1, device_id=(peer(o), h), device_id_type=MESH)
        return 0

    lax.fori_loop(1, ranges, greet, 0)
    pl.semaphore_wait(barrier, ranges - 1 + 3)

    def to_helpers(k, src, dst):
        copies = []
        for d in range(1, 4):
            copies.append(
                pltpu.make_async_remote_copy(
                    src_ref=src,
                    dst_ref=dst.at[h],
                    send_sem=y_send.at[3 * k + d - 1],
                    recv_sem=y_recv.at[3 * k + d - 1],
                    device_id=helper(d),
                    device_id_type=MESH,
                )
            )
        return copies

    y_copies = [to_helpers(0, multi, mall), to_helpers(1, cheb, call), to_helpers(2, idx, iall)]
    for group in y_copies:
        for copy in group:
            copy.start()
    mall[h] = multi[...]
    call[h] = cheb[...]
    iall[h] = idx[...]

    rows = ranges * 8
    step = min(128, rows)
    ghost_b = ghost[...].astype(F32).astype(BF)
    lane64 = iota((step, CAP), 1)
    sub64 = iota((step, CAP), 0) % 8
    lane256 = iota((step, 256), 1)
    low_half = (iota((step, 256), 0) % 8) < 4

    def build_pick(i, _):
        at = pl.multiple_of(i * step, step)
        own = ((iota((step, ranges), 0) + at) // 8) == iota((step, ranges), 1)
        each = dot(jnp.where(own, 1.0, 0.0).astype(BF), ghost_b)

        def chosen(slot):
            one = jnp.sum(jnp.where(lane64 == slot, each, 0.0), axis=1, keepdims=True)
            return lane256 == one.astype(I32)

        def put(ref, col, mask):
            ref[pl.ds(at, step), col : col + 256] = jnp.where(mask, 1.0, 0.0).astype(BF)

        put(pick_f, 0, chosen(16 * h + sub64))
        put(pick_f, 256, chosen(16 * h + 8 + sub64))
        near = chosen(4 * h + sub64 % 4)
        put(pick_n, 0, near & low_half)
        put(pick_n, 256, near & jnp.logical_not(low_half))
        for t in range(4):
            put(pick_e, 256 * t, chosen(16 * h + 4 * t + sub64 % 4) & low_half)
        return 0

    lax.fori_loop(0, rows // step, build_pick, 0)

    for copy in y_copies[0]:
        copy.wait()

    range_multi = mall[...].reshape(256, PW)
    hi, lo = split2(range_multi[:, :128])
    w_pick[0:256, 0:128] = hi
    w_pick[0:256, 128:256] = lo
    messages = step // 8

    def pick_far(i, _):
        at = pl.multiple_of(i * step, step)
        to = pl.ds(i * messages, messages)
        for half in range(2):
            both = dot(pick_f[pl.ds(at, step), 256 * half : 256 * half + 256], w_pick[0:256, :])
            send_f[to, 8 * half : 8 * half + 8, :] = (both[:, :128] + both[:, 128:]).reshape(
                messages, 8, 128
            )
        return 0

    lax.fori_loop(0, rows // step, pick_far, 0)

    def block(s, n):
        return pl.ds(pl.multiple_of(s * n, n), n)

    def exchange(src, dst, s_sem, r_sem, o):
        to = peer(o)
        return pltpu.make_async_remote_copy(
            src_ref=src.at[to],
            dst_ref=dst.at[block(me, src.shape[1]), :],
            send_sem=s_sem.at[o],
            recv_sem=r_sem.at[o],
            device_id=(to, h),
            device_id_type=MESH,
        )

    def send_far(o, _):
        exchange(send_f, recv_f, f_send, f_recv, o).start()
        return 0

    lax.fori_loop(1, ranges, send_far, 0)
    recv_f[block(me, 16), :] = send_f[me]

    tail = jnp.concatenate([range_multi[:, 128:], jnp.zeros((256, 128 - TW), F32)], axis=1)
    hi, lo = split2(tail)
    for t in range(4):
        moved = pltpu.roll(tail, TW * t, axis=1) if t else tail
        hi, lo = split2(moved)
        w_pick[256 * (t + 1) : 256 * (t + 2), 0:128] = hi
        w_pick[256 * (t + 1) : 256 * (t + 2), 128:256] = lo

    for copy in y_copies[1]:
        copy.wait()

    range_cheb = call[...].reshape(256, QW)
    for l in range(5):
        if l < 4:
            part = range_cheb[:, 128 * l : 128 * l + 128]
        else:
            part = jnp.concatenate(
                [range_cheb[:, 512:], jnp.zeros((256, QP - QW), F32)], axis=1
            )
        hi, lo = split2(part)
        w_pick[256 * (l + 5) : 256 * (l + 6), 0:128] = hi
        w_pick[256 * (l + 5) : 256 * (l + 6), 128:256] = lo

    def pick_near(i, _):
        at = pl.multiple_of(i * step, step)
        to = pl.ds(i * messages, messages)
        near = pick_n[pl.ds(at, step), :]
        for half in range(2):
            both = dot(near, w_pick[256 * (5 + 2 * half) : 256 * (7 + 2 * half), :])
            send_n[to, 8 * half : 8 * half + 8, :] = (both[:, :128] + both[:, 128:]).reshape(
                messages, 8, 128
            )
        both = dot(pick_e[pl.ds(at, step), 0:1024], w_pick[256:1280, :])
        both = both + dot(near[:, 256:], w_pick[256 * 9 : 256 * 10, :])
        send_n[to, 16:24, :] = (both[:, :128] + both[:, 128:]).reshape(messages, 8, 128)
        return 0

    lax.fori_loop(0, rows // step, pick_near, 0)

    def send_near(o, _):
        exchange(send_n, recv_n, n_send, n_recv, o).start()
        return 0

    lax.fori_loop(1, ranges, send_near, 0)
    recv_n[block(me, 24), :] = send_n[me]

    for copy in loads:
        copy.wait()
    f_hi[...] = jnp.zeros_like(f_hi)
    f_lo[...] = jnp.zeros_like(f_lo)
    n_hi[...] = jnp.zeros_like(n_hi)
    n_lo[...] = jnp.zeros_like(n_lo)
    t_hi[...] = jnp.zeros_like(t_hi)
    t_lo[...] = jnp.zeros_like(t_lo)

    def split_far_op(k, _):
        hi, lo = split2(ops_f[k])
        f_hi[k, 0:PW, 0:PW] = hi
        f_lo[k, 0:PW, 0:PW] = lo
        return 0

    lax.fori_loop(0, FCLS, split_far_op, 0)

    def split_near_op(k, _):
        hi, lo = split2(ops_n[k])
        n_hi[k, 0:QW, 0:QW] = hi
        n_lo[k, 0:QW, 0:QW] = lo
        return 0

    lax.fori_loop(0, NCLS, split_near_op, 0)
    hi, lo = split2(ops_t[...])
    t_hi[0:PW, 0:QW] = hi
    t_lo[0:PW, 0:QW] = lo

    for copy in y_copies[2]:
        copy.wait()

    lane = iota((BOX, 256), 1)

    def keys(g, _):
        src = iall[g, :, 0:256]
        kind = iall[g, :, 256:512]
        live = kind[:, 255:256]
        is_far = lane < live
        is_near = (lane >= NEAR_AT) & (lane < NEAR_AT + NEAR)
        slot = src - 256
        s = slot >> 6
        c = slot & 63
        own = src < 256
        far_on = jnp.where(own, src >> 6, c >> 4) == h
        c = c & 15
        far_l = jnp.where(own, 128, (c >> 1) * 16) + kind
        far_r = jnp.where(own, src & 63, (c & 1) * 64 + s)
        slot = src - BOX
        s = slot >> 4
        c = slot & 15
        own = src < BOX
        near_on = jnp.where(own, g, c >> 2) == h
        c = c & 3
        near_l = jnp.where(own, 152, 144 + (c >> 1) * 4) + kind
        near_r = jnp.where(own, src, (c & 1) * 64 + s)
        on = (is_near & near_on) | (is_far & far_on)
        left = jnp.where(is_near, near_l, far_l)
        right = jnp.where(is_near, near_r, far_r)
        at = pl.ds(pl.multiple_of(g * BOX, BOX), BOX)
        key_l[at, :] = jnp.where(on, left, -1).astype(F32)
        key_r[at, :] = right.astype(F32)
        return 0

    lax.fori_loop(0, 4, keys, 0)

    sub16 = iota((16, 256), 0).astype(F32).astype(BF)
    unroll = 2

    def count_box(i, _):
        for u in range(unroll):
            b = i * unroll + u
            kl = jnp.broadcast_to(key_l[pl.ds(b, 1), :], (16, 256)).astype(BF)
            kr = jnp.broadcast_to(key_r[pl.ds(b, 1), :], (16, 256)).astype(BF)
            one = jnp.ones((16, 256), BF)
            zero = jnp.zeros((16, 256), BF)
            left = jnp.concatenate(
                [
                    jnp.where(kl == sub16 + jnp.asarray(16 * r, BF), one, zero)
                    for r in range(KEYS // 16)
                ],
                axis=0,
            )
            right = jnp.concatenate(
                [jnp.where(kr == sub16 + jnp.asarray(16 * r, BF), one, zero) for r in range(8)],
                axis=0,
            )
            both = lax.dot_general(
                left, right, (((1,), (1,)), ((), ())), preferred_element_type=F32
            )
            at = pl.ds(pl.multiple_of(b * 16, 16), 16)
            for r in range(9):
                count[at, 128 * r : 128 * r + 128] = both[16 * r : 16 * r + 16, :].astype(BF)
            ncount[at, :] = both[144:160, :]
        return 0

    lax.fori_loop(0, 4 * BOX // unroll, count_box, 0)

    own_cheb = jnp.concatenate([cheb[...], jnp.zeros((BOX, QP - QW), F32)], axis=1)
    own_cheb = jnp.concatenate([own_cheb, jnp.zeros((BOX, QP), F32)], axis=0)
    own_hi, own_lo = split2(own_cheb)

    def near_own(k, _):
        m = ncount[pl.ds(8 + k, 256, stride=16), :].astype(BF)
        near_sum[k] = dot(m, own_hi) + dot(m, own_lo)
        return 0

    lax.fori_loop(0, NCLS, near_own, 0)

    w_main[...] = jnp.zeros_like(w_main)
    w_tail[...] = jnp.zeros_like(w_tail)
    hi, lo = split2(multi[:, 0:128])
    w_main[1024:1088, 0:128] = hi
    w_main[1024:1088, 128:256] = lo

    def put_tail(at, x):
        high = x.astype(BF).astype(F32)
        keep = iota(x.shape, 1) < TW
        packed = jnp.where(keep, high, 0.0) + pltpu.roll(jnp.where(keep, x - high, 0.0), TW, axis=1)
        w_tail[at, :] = packed.astype(BF)

    put_tail(
        pl.ds(1024, BOX),
        jnp.concatenate([multi[:, 128:PW], jnp.zeros((BOX, 128 - TW), F32)], axis=1),
    )

    def far_arrived(o, _):
        exchange(send_f, recv_f, f_send, f_recv, o).wait()
        return 0

    lax.fori_loop(1, ranges, far_arrived, 0)
    for c in range(16):
        hi, lo = split2(recv_f[pl.ds(c, ranges, stride=16), :])
        w_main[64 * c : 64 * c + ranges, 0:128] = hi
        w_main[64 * c : 64 * c + ranges, 128:256] = lo

    def far_rows(i, _):
        at = pl.ds(pl.multiple_of(i * 256, 256), 256)
        both = dot(count[at, :], w_main[...])
        far_main[at, :] = both[:, :128] + both[:, 128:]
        return 0

    lax.fori_loop(0, 16, far_rows, 0)

    def near_arrived(o, _):
        exchange(send_n, recv_n, n_send, n_recv, o).wait()
        return 0

    lax.fori_loop(1, ranges, near_arrived, 0)
    for q in range(4):
        x = recv_n[pl.ds(16 + q, ranges, stride=24), :]
        for t in range(4):
            moved = pltpu.roll(x, 128 - TW * t, axis=1) if t else x
            at = 256 * t + 64 * q
            put_tail(pl.ds(at, ranges), moved)
    if ranges < 64:
        w_near[...] = jnp.zeros_like(w_near)
    for c in range(4):
        for l in range(5):
            row = 4 * l + c if l < 4 else 20 + c
            x = recv_n[pl.ds(row, ranges, stride=24), :]
            hi, lo = split2(x)
            w_near[64 * c : 64 * c + ranges, 128 * l : 128 * l + 128] = hi
            w_near[64 * c : 64 * c + ranges, QP + 128 * l : QP + 128 * l + 128] = lo

    def far_rows_tail(i, _):
        at = pl.ds(pl.multiple_of(i * 256, 256), 256)
        both = dot(count[at, :], w_tail[...])
        far_tail[at, :] = both + pltpu.roll(both, 128 - TW, axis=1)
        return 0

    lax.fori_loop(0, 16, far_rows_tail, 0)

    local_sum[...] = jnp.zeros_like(local_sum)

    def far_class(k, _):
        at = pl.ds(k, 256, stride=16)
        hi, lo = split2(jnp.concatenate([far_main[at, :], far_tail[at, :]], axis=1))
        local_sum[...] += dot(hi, f_hi[k]) + dot(hi, f_lo[k]) + dot(lo, f_hi[k])
        return 0

    lax.fori_loop(0, FCLS, far_class, 0)

    def near_class(k, _):
        m = jnp.concatenate(
            [ncount[pl.ds(k, 256, stride=16), :], ncount[pl.ds(4 + k, 256, stride=16), :]], axis=1
        ).astype(BF)
        total = near_sum[k] + dot(m, w_near[:, 0:QP]) + dot(m, w_near[:, QP:])
        hi, lo = split2(total)
        nh[k] = hi
        nl[k] = lo
        return 0

    lax.fori_loop(0, NCLS, near_class, 0)

    lh, ll = split2(local_sum[...])
    back = []
    for n, (n0, w) in enumerate(((0, 256), (256, 256), (512, 128))):
        cols = slice(n0, n0 + w)
        total = dot(lh, t_hi[:, cols]) + dot(lh, t_lo[:, cols]) + dot(ll, t_hi[:, cols])
        for k in range(NCLS):
            total = total + (
                dot(nh[k], n_hi[k, :, cols])
                + dot(nh[k], n_lo[k, :, cols])
                + dot(nl[k], n_hi[k, :, cols])
            )
        rs_send[:, :, cols] = total.reshape(4, BOX, w)
        for d in (2, 1, 3):
            copy = pltpu.make_async_remote_copy(
                src_ref=rs_send.at[(h + d) % 4, :, cols],
                dst_ref=rs_recv.at[d - 1, :, cols],
                send_sem=r_send.at[3 * n + d - 1],
                recv_sem=r_recv.at[3 * n + d - 1],
                device_id=helper(d),
                device_id_type=MESH,
            )
            copy.start()
            back.append(copy)
    for copy in back:
        copy.wait()
    total = rs_send[h] + rs_recv[0] + rs_recv[1] + rs_recv[2]
    out[...] = total[:, :QW]


def shards(sizes, multi, cheb, ghost, far_src, far_kind, far_count, near_src, near_kind, far_ops, near_ops, to_target):
    ranges = sizes[0] * sizes[1] * sizes[2]

    def lanes(far, near, last):
        gap = jnp.zeros((BOX, NEAR_AT - FAR), I32)
        rest = jnp.zeros((BOX, 255 - NEAR_AT - NEAR), I32)
        return jnp.concatenate([far, gap, near, rest, last], axis=1)

    idx = jnp.concatenate(
        [
            lanes(far_src, near_src, jnp.zeros((BOX, 1), I32)),
            lanes(far_kind, near_kind, far_count[:, None]),
        ],
        axis=1,
    )
    rows = ranges * 8
    vmem = pl.BlockSpec(memory_space=pltpu.VMEM)
    hbm = pl.BlockSpec(memory_space=pl.ANY)
    dma = pltpu.SemaphoreType.DMA
    return pl.pallas_call(
        functools.partial(evaluate, sizes),
        out_shape=jax.ShapeDtypeStruct((BOX, QW), F32),
        in_specs=[vmem] * 4 + [hbm] * 3,
        out_specs=vmem,
        scratch_shapes=[
            pltpu.VMEM((4, BOX, PW), F32),
            pltpu.VMEM((4, BOX, QW), F32),
            pltpu.VMEM((4, BOX, 512), I32),
            pltpu.VMEM((ranges, 16, 128), F32),
            pltpu.VMEM((ranges, 24, 128), F32),
            pltpu.VMEM((ranges * 16, 128), F32),
            pltpu.VMEM((ranges * 24, 128), F32),
            pltpu.VMEM((rows, 512), BF),
            pltpu.VMEM((rows, 512), BF),
            pltpu.VMEM((rows, 1024), BF),
            pltpu.VMEM((2560, 256), BF),
            pltpu.VMEM((256, 256), F32),
            pltpu.VMEM((256, 256), F32),
            pltpu.VMEM((4096, SW), BF),
            pltpu.VMEM((4096, 128), F32),
            pltpu.VMEM((SW, 256), BF),
            pltpu.VMEM((SW, 128), BF),
            pltpu.VMEM((256, 2 * QP), BF),
            pltpu.VMEM((4096, 128), F32),
            pltpu.VMEM((4096, 128), F32),
            pltpu.VMEM((FCLS, PW, PW), F32),
            pltpu.VMEM((NCLS, QW, QW), F32),
            pltpu.VMEM((PW, QW), F32),
            pltpu.VMEM((FCLS, 256, 256), BF),
            pltpu.VMEM((FCLS, 256, 256), BF),
            pltpu.VMEM((NCLS, QP, QP), BF),
            pltpu.VMEM((NCLS, QP, QP), BF),
            pltpu.VMEM((256, QP), BF),
            pltpu.VMEM((256, QP), BF),
            pltpu.VMEM((256, 256), F32),
            pltpu.VMEM((NCLS, 256, QP), F32),
            pltpu.VMEM((NCLS, 256, QP), BF),
            pltpu.VMEM((NCLS, 256, QP), BF),
            pltpu.VMEM((4, BOX, QP), F32),
            pltpu.VMEM((3, BOX, QP), F32),
            dma((9,)),
            dma((9,)),
            dma((ranges,)),
            dma((ranges,)),
            dma((ranges,)),
            dma((ranges,)),
            dma((9,)),
            dma((9,)),
            dma((3,)),
        ],
        compiler_params=pltpu.CompilerParams(
            collective_id=0, has_side_effects=True, vmem_limit_bytes=60 * 1024 * 1024
        ),
        name="evaluate",
    )(multi, cheb, ghost, idx, far_ops, near_ops, to_target)


def solution(mesh, sizes=(4, 8, 2)):
    rows = P(("morton", "grp"), None)
    placed = (
        rows,
        rows,
        P("morton", None),
        rows,
        rows,
        P(("morton", "grp")),
        rows,
        rows,
        P(),
        P(),
        P(),
    )
    return jax.shard_map(
        functools.partial(shards, sizes), mesh=mesh, in_specs=placed, out_specs=rows, check_vma=False
    )
```

time: 332 us -> 102 us (0.31)
  other arithmetic: 186 us -> 0 us
  blocking collectives: 97.9 us -> 0 us
  Pallas kernels: 0 us -> 96.2 us
  between operations: 13.6 us -> 0.03 us
  local copies, waits for them, and re-layouts: 17.4 us -> 5.61 us
  matrix products: 11.2 us -> 0 us
  waiting for transfers between devices: 4.05 us -> 0 us
    scatter-add x2 -> x0, other arithmetic: 178 us -> none  [class_sum(): jax.ops.segment_sum(picked.reshape(targets * slot_count, lookup.shape[1])...]
    pallas_call x0 -> x1, Pallas kernels: none -> 96.2 us  [shards(): pl.pallas_call(functools.partial(evaluate, sizes), out_shape=jax.ShapeDty...]
    all_to_all x4 -> x0, blocking collectives: 74.9 us -> none  [turned_blocks(): lax.all_to_all(tiles, axes[k], split_axis=k, concat_axis=k, tiled=True)]
    all_gather x2 -> x0, blocking collectives: 23 us -> none  [the longest x1 13.1 us: shards(): lax.all_gather(chebyshev, 'grp', axis=0, tiled=True)]
    dot_general x3 -> x0, matrix products: 11.2 us -> none  [the longest x1 6.76 us: evaluate(): jnp.einsum('tkc,kcd->td', near_sum, near_ops, precision=lax.Precision.HIG...]
    gather x2 -> x0, local copies, waits for them, and re-layouts: 6.56 us -> none  [the longest x1 4.65 us: shards(): range_multi[far_chosen]]
    concatenate x2 -> x0, other arithmetic: 6.3 us -> none  [the longest x1 4.57 us: shards(): jnp.concatenate([range_multi, ghost_multi.reshape(-1, width_p)], axis=0)]
    all_gather x2 -> x0, waiting for transfers between devices: 4.02 us -> none  [the longest x1 4.02 us: shards(): lax.all_gather(ghost_multi, 'grp', axis=1, tiled=True)]
  transfers between devices with their start and end apart: 2 -> 0, of which waited for: 1 -> 0; matrix products, arithmetic and copies ran while one was open for 16% -> 0% of each run, Pallas kernels for 0% -> 0%
where the time goes in v1:
time: 102 us
  Pallas kernels  96.2 us (94%)
  local copies, waits for them, and re-layouts  5.61 us (6%)
    pallas_call x1, Pallas kernels, shards(): pl.pallas_call(functools.partial(evaluate, sizes), out_shape=jax.ShapeDty...  96.2 us
    unnamed x3, local copies, waits for them, and re-layouts  3.19 us

profile of v1, /device:TPU:1, one launch (start us, length us, event | category | flops | bytes accessed | tf_op | source)
XLA Modules:
  0.0 101.8 jit_solution(4568204809890818230)
XLA Ops:
  0.0 0.7 copy.14
  0.7 0.8 copy.12
  1.5 0.8 copy.13
  2.4 1.7 %concatenate.3.idx = s32[64,512]{1,0:T(8,128)} concatenate(s32[64,189]{1,0:T(8,128)} %param.14, s32[64,3]{1,0:T(8,128)S(1)} %broadcast.6, s32[64,27]{1,0:T(8,128)S(1)} %copy.12, s32[64,36]{1,0:T(8,128)S(1)} %broadcast.7, s32[64,1]{1,0:T(8,128)S(1)} %broadcast_in_dim.6, s32[64,189]{1,0:T(8,128)} %param.15, s32[64,3]{1,0:T(8,128)S(1)} %broadcast.6, s32[64,27]{1,0:T(8,128)S(1)} %copy.13, ...), dimensions={1} | concatenate | bytes 262144 | tf_op jit(solution)/shard_map/concatenate | solution.py:511
  4.0 96.2 %evaluate.1 = f32[64,560]{1,0:T(8,128)} custom-call(f32[64,152]{1,0:T(8,128)} %multi.1, f32[64,560]{1,0:T(8,128)} %cheb.1, s32[64,64]{1,0:T(8,128)} %ghost.1, s32[64,512]{1,0:T(8,128)} %concatenate.3.idx, f32[16,152,152]{2,1,0:T(8,128)} %far_ops.1, f32[4,560,560]{2,1,0:T(8,128)} %near_ops.1, f32[152,560]{1,0:T(8,128)} %to_target.1), custom_call_target="tpu_custom_call" | custom-call | tf_op jit(solution)/shard_map/evaluate/pallas_call | solution.py:522
  100.2 1.6 %copy.16 = f32[64,560]{1,0:T(8,128)} copy(f32[64,560]{1,0:T(8,128)} %evaluate.1) | data formatting | bytes 286720
  (3 shorter events, 0.0 us)

commit v2 on v1

v2 whole, which is shorter than its diff:
```python
import functools

import jax
import jax.numpy as jnp
from jax import lax
from jax.experimental import pallas as pl
from jax.experimental.pallas import tpu as pltpu
from jax.sharding import PartitionSpec as P

MESH = pl.DeviceIdType.MESH
BF = jnp.bfloat16
F32 = jnp.float32
I32 = jnp.int32

PW = 152
TW = PW - 128
QW = 560
QP = 640
FAR = 189
NEAR = 27
NEAR_AT = 192
CAP = 64
NCAP = 16
FCLS = 16
NCLS = 4
BOX = 64
KEYS = 160
SW = 1152


def split2(x):
    hi = x.astype(BF)
    return hi, (x - hi.astype(F32)).astype(BF)


def dot(a, b):
    return jnp.dot(a, b, preferred_element_type=F32)


def iota(shape, dim):
    return lax.broadcasted_iota(I32, shape, dim)


def evaluate(
    sizes,
    multi,
    cheb,
    ghost,
    far_src,
    far_kind,
    far_count,
    near_src,
    near_kind,
    far_ops,
    near_ops,
    to_target,
    out,
    mall,
    call,
    iall,
    send_f,
    send_n,
    recv_f,
    recv_n,
    pick_f,
    pick_n,
    pick_e,
    w_pick,
    turned,
    key_l,
    key_r,
    count,
    ncount,
    w_main,
    w_tail,
    w_near,
    far_main,
    far_tail,
    ops_f,
    ops_n,
    ops_t,
    f_hi,
    f_lo,
    n_hi,
    n_lo,
    t_hi,
    t_lo,
    local_sum,
    near_sum,
    parts,
    rs_send,
    rs_recv,
    y_send,
    y_recv,
    f_send,
    f_recv,
    n_send,
    n_recv,
    r_send,
    r_recv,
    load,
):
    xs, zs, cs = sizes
    ranges = xs * zs * cs
    me = lax.axis_index("morton")
    h = lax.axis_index("grp")
    my_x = lax.div(me, zs * cs)
    my_z = lax.rem(lax.div(me, cs), zs)
    my_c = lax.rem(me, cs)

    def helper(d):
        return (me, lax.rem(h + d, 4))

    def peer(o):
        zz = lax.rem(o, zs)
        up = lax.div(zz + 1, 2)
        dz = up + lax.rem(zz + 1, 2) * (zs - 2 * up)
        dx = lax.rem(lax.div(o, zs), xs)
        dc = lax.div(o, zs * xs)
        x = lax.rem(my_x + dx, xs)
        z = lax.rem(my_z + dz, zs)
        return (x * zs + z) * cs + lax.rem(my_c + dc, cs)

    loads = [
        pltpu.make_async_copy(far_ops, ops_f, load.at[0]),
        pltpu.make_async_copy(near_ops, ops_n, load.at[1]),
        pltpu.make_async_copy(to_target, ops_t, load.at[2]),
    ]
    for copy in loads:
        copy.start()

    lane64 = iota((BOX, 128), 1)
    tail = jnp.concatenate([multi[:, 128:], jnp.zeros((BOX, 128 - TW), F32)], axis=1)
    rest = jnp.concatenate([cheb[:, 512:], jnp.zeros((BOX, QP - QW), F32)], axis=1)
    mall[h] = multi[:, 0:128]
    call[h, :, 0:512] = cheb[:, 0:512]
    call[h, :, 512:QP] = rest + pltpu.roll(tail, QW - 512, axis=1)
    turned[...] = jnp.zeros_like(turned)
    turned[0:NEAR, 0:BOX] = near_src[...].astype(F32)
    turned[32 : 32 + NEAR, 0:BOX] = near_kind[...].astype(F32)
    turned[64:65, 0:BOX] = far_count[...].astype(F32)
    near = turned[...].T[0:BOX, :]
    at_near = (lane64 >= 64) & (lane64 < 64 + NEAR)

    def second(far, shift):
        far = jnp.concatenate([far[:, 128:], jnp.zeros((BOX, 256 - FAR), I32)], axis=1)
        moved = pltpu.roll(near, shift, axis=1).astype(I32)
        return jnp.where(at_near, moved, jnp.where(lane64 < FAR - 128, far, 0))

    iall[h, :, 0:128] = far_src[:, 0:128]
    iall[h, :, 128:256] = second(far_src, 64)
    iall[h, :, 256:384] = far_kind[:, 0:128]
    live = pltpu.roll(near, 63, axis=1).astype(I32)
    iall[h, :, 384:512] = jnp.where(lane64 == 127, live, second(far_kind, 32))

    barrier = pltpu.get_barrier_semaphore()
    for d in range(1, 4):
        pl.semaphore_signal(barrier, inc=1, device_id=helper(d), device_id_type=MESH)

    def greet(o, _):
        pl.semaphore_signal(barrier, inc=1, device_id=(peer(o), h), device_id_type=MESH)
        return 0

    lax.fori_loop(1, ranges, greet, 0)

    rows = ranges * 8
    step = min(128, rows)
    ghost_b = ghost[...].astype(F32).astype(BF)
    lane_c = iota((step, CAP), 1)
    sub = iota((step, CAP), 0) % 8
    lane256 = iota((step, 256), 1)
    low_half = (iota((step, 256), 0) % 8) < 4

    def build_pick(i, _):
        at = pl.multiple_of(i * step, step)
        own = ((iota((step, ranges), 0) + at) // 8) == iota((step, ranges), 1)
        each = dot(jnp.where(own, 1.0, 0.0).astype(BF), ghost_b)

        def chosen(slot):
            one = jnp.sum(jnp.where(lane_c == slot, each, 0.0), axis=1, keepdims=True)
            return lane256 == one.astype(I32)

        def put(ref, col, mask):
            ref[pl.ds(at, step), col : col + 256] = jnp.where(mask, 1.0, 0.0).astype(BF)

        put(pick_f, 0, chosen(16 * h + sub))
        put(pick_f, 256, chosen(16 * h + 8 + sub))
        near = chosen(4 * h + sub % 4)
        put(pick_n, 0, near & low_half)
        put(pick_n, 256, near & jnp.logical_not(low_half))
        for t in range(4):
            put(pick_e, 256 * t, chosen(16 * h + 4 * t + sub % 4) & low_half)
        return 0

    lax.fori_loop(0, rows // step, build_pick, 0)

    for copy in loads:
        copy.wait()
    for ref in (f_hi, f_lo, n_hi, n_lo, t_hi, t_lo, near_sum, w_main, w_tail):
        ref[...] = jnp.zeros_like(ref)

    def split_far_op(k, _):
        hi, lo = split2(ops_f[k])
        at = pl.ds(pl.multiple_of(k * 256, 256), PW)
        f_hi[at, 0:PW] = hi
        f_lo[at, 0:PW] = lo
        return 0

    lax.fori_loop(0, FCLS, split_far_op, 0)

    def split_near_op(k, _):
        hi, lo = split2(ops_n[k])
        at = pl.ds(pl.multiple_of(k * QP, QP), QW)
        n_hi[at, 0:QW] = hi
        n_lo[at, 0:QW] = lo
        return 0

    lax.fori_loop(0, NCLS, split_near_op, 0)
    hi, lo = split2(ops_t[...])
    t_hi[0:PW, 0:QW] = hi
    t_lo[0:PW, 0:QW] = lo

    pl.semaphore_wait(barrier, ranges - 1 + 3)

    def to_helpers(k, ref):
        copies = []
        for d in (2, 1, 3):
            copies.append(
                pltpu.make_async_remote_copy(
                    src_ref=ref.at[h],
                    dst_ref=ref.at[h],
                    send_sem=y_send.at[3 * k + d - 1],
                    recv_sem=y_recv.at[3 * k + d - 1],
                    device_id=helper(d),
                    device_id_type=MESH,
                )
            )
        return copies

    y_copies = [to_helpers(0, mall), to_helpers(1, call), to_helpers(2, iall)]
    for group in y_copies:
        for copy in group:
            copy.start()

    lane = iota((BOX, 256), 1)

    def keys(g):
        src = iall[g, :, 0:256]
        kind = iall[g, :, 256:512]
        live = kind[:, 255:256]
        is_far = (lane < live) & (lane < FAR)
        is_near = (lane >= NEAR_AT) & (lane < NEAR_AT + NEAR)
        slot = src - 256
        s = slot >> 6
        c = slot & 63
        own = src < 256
        far_on = jnp.where(own, src >> 6, c >> 4) == h
        c = c & 15
        far_l = jnp.where(own, 128, (c >> 1) * 16) + kind
        far_r = jnp.where(own, src & 63, (c & 1) * 64 + s)
        slot = src - BOX
        s = slot >> 4
        c = slot & 15
        own = src < BOX
        near_on = jnp.where(own, g, c >> 2) == h
        c = c & 3
        near_l = jnp.where(own, 152, 144 + (c >> 1) * 4) + kind
        near_r = jnp.where(own, src, (c & 1) * 64 + s)
        on = (is_near & near_on) | (is_far & far_on)
        left = jnp.where(is_near, near_l, far_l)
        right = jnp.where(is_near, near_r, far_r)
        at = pl.ds(pl.multiple_of(g * BOX, BOX), BOX)
        key_l[at, :] = jnp.where(on, left, -1).astype(F32)
        key_r[at, :] = right.astype(F32)

    sub16 = iota((16, 256), 0).astype(F32).astype(BF)
    unroll = 8

    def count_box(b):
        kl = jnp.broadcast_to(key_l[pl.ds(b, 1), :], (16, 256)).astype(BF)
        kr = jnp.broadcast_to(key_r[pl.ds(b, 1), :], (16, 256)).astype(BF)
        one = jnp.ones((16, 256), BF)
        zero = jnp.zeros((16, 256), BF)
        left = jnp.concatenate(
            [
                jnp.where(kl == sub16 + jnp.asarray(16 * r, BF), one, zero)
                for r in range(KEYS // 16)
            ],
            axis=0,
        )
        right = jnp.concatenate(
            [jnp.where(kr == sub16 + jnp.asarray(16 * r, BF), one, zero) for r in range(8)],
            axis=0,
        )
        return lax.dot_general(
            left, right, (((1,), (1,)), ((), ())), preferred_element_type=F32
        )

    def count_block(g):
        def some(i, _):
            first = g * BOX + i * unroll
            found = [count_box(first + u) for u in range(unroll)]
            for u, both in enumerate(found):
                at = pl.ds(pl.multiple_of((first + u) * 16, 16), 16)
                for r in range(9):
                    count[at, 128 * r : 128 * r + 128] = both[16 * r : 16 * r + 16, :].astype(BF)
                ncount[at, :] = both[144:160, :]
            return 0

        lax.fori_loop(0, BOX // unroll, some, 0)

    keys(h)
    count_block(h)

    for copy in y_copies[0]:
        copy.wait()

    hi, lo = split2(mall[...].reshape(256, 128))
    w_pick[0:256, 0:128] = hi
    w_pick[0:256, 128:256] = lo
    messages = step // 8

    def pick_far(i, _):
        at = pl.multiple_of(i * step, step)
        to = pl.ds(i * messages, messages)
        for half in range(2):
            both = dot(pick_f[pl.ds(at, step), 256 * half : 256 * half + 256], w_pick[0:256, :])
            send_f[to, 8 * half : 8 * half + 8, :] = (both[:, :128] + both[:, 128:]).reshape(
                messages, 8, 128
            )
        return 0

    lax.fori_loop(0, rows // step, pick_far, 0)

    def block(s, n):
        return pl.ds(pl.multiple_of(s * n, n), n)

    def exchange(src, dst, s_sem, r_sem, o):
        to = peer(o)
        return pltpu.make_async_remote_copy(
            src_ref=src.at[to],
            dst_ref=dst.at[block(me, src.shape[1]), :],
            send_sem=s_sem.at[o],
            recv_sem=r_sem.at[o],
            device_id=(to, h),
            device_id_type=MESH,
        )

    def send_far(o, _):
        exchange(send_f, recv_f, f_send, f_recv, o).start()
        return 0

    lax.fori_loop(1, ranges, send_far, 0)
    recv_f[block(me, 16), :] = send_f[me]

    own_cheb = jnp.concatenate([cheb[:, 0:512], rest], axis=1)
    own_cheb = jnp.concatenate([own_cheb, jnp.zeros((BOX, QP), F32)], axis=0)
    own_hi, own_lo = split2(own_cheb)
    mine = pl.ds(pl.multiple_of(h * BOX, BOX), BOX)
    for k in range(NCLS):
        m = ncount[pl.ds(h * 16 * BOX + 8 + k, BOX, stride=16), :].astype(BF)
        near_sum[k, mine, :] = dot(m, own_hi) + dot(m, own_lo)

    hi, lo = split2(multi[:, 0:128])
    w_main[1024:1088, 0:128] = hi
    w_main[1024:1088, 128:256] = lo

    def put_tail(at, x):
        high = x.astype(BF).astype(F32)
        keep = iota(x.shape, 1) < TW
        packed = jnp.where(keep, high, 0.0) + pltpu.roll(jnp.where(keep, x - high, 0.0), TW, axis=1)
        w_tail[at, :] = packed.astype(BF)

    put_tail(pl.ds(1024, BOX), tail)

    for copy in y_copies[1]:
        copy.wait()

    lane_t = iota((256, 128), 1)
    last = call[:, :, 512:QP].reshape(256, 128)
    tails = jnp.where(lane_t < TW, pltpu.roll(last, 128 - (QW - 512), axis=1), 0.0)
    for t in range(4):
        hi, lo = split2(pltpu.roll(tails, TW * t, axis=1) if t else tails)
        w_pick[256 * (t + 1) : 256 * (t + 2), 0:128] = hi
        w_pick[256 * (t + 1) : 256 * (t + 2), 128:256] = lo
    for l in range(5):
        if l < 4:
            part = call[:, :, 128 * l : 128 * l + 128].reshape(256, 128)
        else:
            part = jnp.where(lane_t < QW - 512, last, 0.0)
        hi, lo = split2(part)
        w_pick[256 * (l + 5) : 256 * (l + 6), 0:128] = hi
        w_pick[256 * (l + 5) : 256 * (l + 6), 128:256] = lo

    def pick_near(i, _):
        at = pl.multiple_of(i * step, step)
        to = pl.ds(i * messages, messages)
        near = pick_n[pl.ds(at, step), :]
        for half in range(2):
            both = dot(near, w_pick[256 * (5 + 2 * half) : 256 * (7 + 2 * half), :])
            send_n[to, 8 * half : 8 * half + 8, :] = (both[:, :128] + both[:, 128:]).reshape(
                messages, 8, 128
            )
        both = dot(pick_e[pl.ds(at, step), 0:1024], w_pick[256:1280, :])
        both = both + dot(near[:, 256:], w_pick[256 * 9 : 256 * 10, :])
        send_n[to, 16:24, :] = (both[:, :128] + both[:, 128:]).reshape(messages, 8, 128)
        return 0

    lax.fori_loop(0, rows // step, pick_near, 0)

    def send_near(o, _):
        exchange(send_n, recv_n, n_send, n_recv, o).start()
        return 0

    lax.fori_loop(1, ranges, send_near, 0)
    recv_n[block(me, 24), :] = send_n[me]

    for copy in y_copies[2]:
        copy.wait()

    def other_block(d, _):
        g = lax.rem(h + d, 4)
        keys(g)
        count_block(g)
        return 0

    lax.fori_loop(1, 4, other_block, 0)

    def far_arrived(o, _):
        exchange(send_f, recv_f, f_send, f_recv, o).wait()
        return 0

    lax.fori_loop(1, ranges, far_arrived, 0)
    for c in range(16):
        hi, lo = split2(recv_f[pl.ds(c, ranges, stride=16), :])
        w_main[64 * c : 64 * c + ranges, 0:128] = hi
        w_main[64 * c : 64 * c + ranges, 128:256] = lo

    tall = 1024

    def far_rows(i, _):
        at = pl.ds(pl.multiple_of(i * tall, tall), tall)
        both = dot(count[at, :], w_main[...])
        far_main[at, :] = both[:, :128] + both[:, 128:]
        return 0

    lax.fori_loop(0, 4096 // tall, far_rows, 0)

    def near_arrived(o, _):
        exchange(send_n, recv_n, n_send, n_recv, o).wait()
        return 0

    lax.fori_loop(1, ranges, near_arrived, 0)
    for q in range(4):
        x = recv_n[pl.ds(16 + q, ranges, stride=24), :]
        for t in range(4):
            moved = pltpu.roll(x, 128 - TW * t, axis=1) if t else x
            at = 256 * t + 64 * q
            put_tail(pl.ds(at, ranges), moved)
    if ranges < 64:
        w_near[...] = jnp.zeros_like(w_near)
    for c in range(4):
        for l in range(5):
            row = 4 * l + c if l < 4 else 20 + c
            x = recv_n[pl.ds(row, ranges, stride=24), :]
            hi, lo = split2(x)
            w_near[64 * c : 64 * c + ranges, 128 * l : 128 * l + 128] = hi
            w_near[64 * c : 64 * c + ranges, QP + 128 * l : QP + 128 * l + 128] = lo

    def far_rows_tail(i, _):
        at = pl.ds(pl.multiple_of(i * tall, tall), tall)
        both = dot(count[at, :], w_tail[...])
        far_tail[at, :] = both + pltpu.roll(both, 128 - TW, axis=1)
        return 0

    lax.fori_loop(0, 4096 // tall, far_rows_tail, 0)

    for k in range(NCLS):
        m = jnp.concatenate(
            [ncount[pl.ds(k, 256, stride=16), :], ncount[pl.ds(4 + k, 256, stride=16), :]], axis=1
        ).astype(BF)
        hi, lo = split2(near_sum[k] + dot(m, w_near[:, 0:QP]) + dot(m, w_near[:, QP:]))
        parts[0:256, QP * k : QP * k + QP] = hi
        parts[256:512, QP * k : QP * k + QP] = lo

    group = 4
    local_sum[...] = jnp.zeros_like(local_sum)

    def far_class(i, _):
        his, los = [], []
        for k in range(group):
            at = pl.ds(i * group + k, 256, stride=16)
            for ref in (far_main, far_tail):
                hi, lo = split2(ref[at, :])
                his.append(hi)
                los.append(lo)
        high = jnp.concatenate(his, axis=1)
        at = pl.ds(pl.multiple_of(i * 256 * group, 256), 256 * group)
        both = dot(jnp.concatenate([high, jnp.concatenate(los, axis=1)], axis=0), f_hi[at, :])
        local_sum[...] += both[0:256] + both[256:512] + dot(high, f_lo[at, :])
        return 0

    lax.fori_loop(0, FCLS // group, far_class, 0)

    lh, ll = split2(local_sum[...])
    local_parts = jnp.concatenate([lh, ll], axis=0)
    back = []
    for n, (n0, w) in enumerate(((0, 256), (256, 256), (512, 128))):
        cols = slice(n0, n0 + w)
        both = dot(parts[...], n_hi[:, cols]) + dot(local_parts, t_hi[:, cols])
        total = both[0:256] + both[256:512]
        total = total + dot(parts[0:256, :], n_lo[:, cols]) + dot(lh, t_lo[:, cols])
        rs_send[:, :, cols] = total.reshape(4, BOX, w)
        for d in (2, 1, 3):
            copy = pltpu.make_async_remote_copy(
                src_ref=rs_send.at[lax.rem(h + d, 4), :, cols],
                dst_ref=rs_recv.at[d - 1, :, cols],
                send_sem=r_send.at[3 * n + d - 1],
                recv_sem=r_recv.at[3 * n + d - 1],
                device_id=helper(d),
                device_id_type=MESH,
            )
            copy.start()
            back.append(copy)
    for copy in back:
        copy.wait()
    total = rs_send[h] + rs_recv[0] + rs_recv[1] + rs_recv[2]
    out[...] = total[:, :QW]


def shards(sizes, multi, cheb, ghost, far_src, far_kind, far_count, near_src, near_kind, far_ops, near_ops, to_target):
    ranges = sizes[0] * sizes[1] * sizes[2]

    rows = ranges * 8
    vmem = pl.BlockSpec(memory_space=pltpu.VMEM)
    hbm = pl.BlockSpec(memory_space=pl.ANY)
    dma = pltpu.SemaphoreType.DMA
    return pl.pallas_call(
        functools.partial(evaluate, sizes),
        out_shape=jax.ShapeDtypeStruct((BOX, QW), F32),
        in_specs=[vmem] * 8 + [hbm] * 3,
        out_specs=vmem,
        scratch_shapes=[
            pltpu.VMEM((4, BOX, 128), F32),
            pltpu.VMEM((4, BOX, QP), F32),
            pltpu.VMEM((4, BOX, 512), I32),
            pltpu.VMEM((ranges, 16, 128), F32),
            pltpu.VMEM((ranges, 24, 128), F32),
            pltpu.VMEM((ranges * 16, 128), F32),
            pltpu.VMEM((ranges * 24, 128), F32),
            pltpu.VMEM((rows, 512), BF),
            pltpu.VMEM((rows, 512), BF),
            pltpu.VMEM((rows, 1024), BF),
            pltpu.VMEM((2560, 256), BF),
            pltpu.VMEM((128, 128), F32),
            pltpu.VMEM((256, 256), F32),
            pltpu.VMEM((256, 256), F32),
            pltpu.VMEM((4096, SW), BF),
            pltpu.VMEM((4096, 128), F32),
            pltpu.VMEM((SW, 256), BF),
            pltpu.VMEM((SW, 128), BF),
            pltpu.VMEM((256, 2 * QP), BF),
            pltpu.VMEM((4096, 128), F32),
            pltpu.VMEM((4096, 128), F32),
            pltpu.VMEM((FCLS, PW, PW), F32),
            pltpu.VMEM((NCLS, QW, QW), F32),
            pltpu.VMEM((PW, QW), F32),
            pltpu.VMEM((FCLS * 256, 256), BF),
            pltpu.VMEM((FCLS * 256, 256), BF),
            pltpu.VMEM((NCLS * QP, QP), BF),
            pltpu.VMEM((NCLS * QP, QP), BF),
            pltpu.VMEM((256, QP), BF),
            pltpu.VMEM((256, QP), BF),
            pltpu.VMEM((256, 256), F32),
            pltpu.VMEM((NCLS, 256, QP), F32),
            pltpu.VMEM((512, NCLS * QP), BF),
            pltpu.VMEM((4, BOX, QP), F32),
            pltpu.VMEM((3, BOX, QP), F32),
            dma((9,)),
            dma((9,)),
            dma((ranges,)),
            dma((ranges,)),
            dma((ranges,)),
            dma((ranges,)),
            dma((9,)),
            dma((9,)),
            dma((3,)),
        ],
        compiler_params=pltpu.CompilerParams(
            collective_id=0, has_side_effects=True, vmem_limit_bytes=60 * 1024 * 1024
        ),
        name="evaluate",
    )(
        multi,
        cheb,
        ghost,
        far_src,
        far_kind,
        far_count.reshape(1, BOX),
        near_src.T,
        near_kind.T,
        far_ops,
        near_ops,
        to_target,
    )


def solution(mesh, sizes=(4, 8, 2)):
    rows = P(("morton", "grp"), None)
    placed = (
        rows,
        rows,
        P("morton", None),
        rows,
        rows,
        P(("morton", "grp")),
        rows,
        rows,
        P(),
        P(),
        P(),
    )
    return jax.shard_map(
        functools.partial(shards, sizes), mesh=mesh, in_specs=placed, out_specs=rows, check_vma=False
    )
```

time: 102 us -> 73.9 us (0.72)
  Pallas kernels: 96.2 us -> 72.2 us
  local copies, waits for them, and re-layouts: 5.61 us -> 1.59 us
    pallas_call x1, Pallas kernels: 96.2 us -> 72.2 us  [shards(): pl.pallas_call(functools.partial(evaluate, sizes), out_shape=jax.ShapeDty...]
    concatenate x1 -> x0, local copies, waits for them, and re-layouts: 1.66 us -> none  [shards(): jnp.concatenate([lanes(far_src, near_src, jnp.zeros((BOX, 1), I32)), lane...]
    unnamed x3 -> x1, local copies, waits for them, and re-layouts: 3.19 us -> 1.59 us
where the time goes in v2:
time: 73.9 us; the launch traced here: 73.8 us
  Pallas kernels  72.2 us (98%)
  local copies, waits for them, and re-layouts  1.59 us (2%)
    pallas_call x1, Pallas kernels, shards(): pl.pallas_call(functools.partial(evaluate, sizes), out_shape=jax.ShapeDty...  72.2 us
    unnamed x1, local copies, waits for them, and re-layouts  1.59 us

profile of v2, /device:TPU:1, one launch (start us, length us, event | category | flops | bytes accessed | tf_op | source)
XLA Modules:
  0.0 73.8 jit_solution(12097617211443055393)
XLA Ops:
  0.0 72.2 %evaluate.1 = f32[64,560]{1,0:T(8,128)} custom-call(f32[64,152]{1,0:T(8,128)} %multi.1, f32[64,560]{1,0:T(8,128)} %cheb.1, s32[64,64]{1,0:T(8,128)} %ghost.1, s32[64,189]{1,0:T(8,128)} %far_src.1, s32[64,189]{1,0:T(8,128)} %far_kind.1, s32[1,64]{1,0:T(1,128)} %bitcast.5, s32[27,64]{1,0:T(8,128)} %bitcast.3, s32[27,64]{1,0:T(8,128)} %bitcast.4, ...), custom_call_target="tpu_custom_call" | custom-call | tf_op jit(solution)/shard_map/evaluate/pallas_call | solution.py:538
  72.2 1.6 %copy.13 = f32[64,560]{1,0:T(8,128)} copy(f32[64,560]{1,0:T(8,128)} %evaluate.1) | data formatting | bytes 286720

commit v3 on v2

--- a/solution.py
+++ b/solution.py
@@ -43,6 +43,18 @@
 
 def evaluate(
     sizes,
+    multi_in,
+    cheb_in,
+    ghost_in,
+    far_src_in,
+    far_kind_in,
+    far_count_in,
+    near_src_in,
+    near_kind_in,
+    far_ops,
+    near_ops,
+    to_target,
+    out,
     multi,
     cheb,
     ghost,
@@ -51,17 +63,15 @@
     far_count,
     near_src,
     near_kind,
-    far_ops,
-    near_ops,
-    to_target,
-    out,
     mall,
     call,
     iall,
     send_f,
     send_n,
+    send_e,
     recv_f,
     recv_n,
+    recv_e,
     pick_f,
     pick_n,
     pick_e,
@@ -87,18 +97,24 @@
     t_lo,
     local_sum,
     near_sum,
+    total_far,
     parts,
     rs_send,
     rs_recv,
+    fold,
+    fold_recv,
     y_send,
     y_recv,
     f_send,
     f_recv,
     n_send,
     n_recv,
+    e_send,
+    e_recv,
     r_send,
     r_recv,
     load,
+    small,
 ):
     xs, zs, cs = sizes
     ranges = xs * zs * cs
@@ -111,21 +127,53 @@
     def helper(d):
         return (me, lax.rem(h + d, 4))
 
-    def peer(o):
-        zz = lax.rem(o, zs)
-        up = lax.div(zz + 1, 2)
-        dz = up + lax.rem(zz + 1, 2) * (zs - 2 * up)
-        dx = lax.rem(lax.div(o, zs), xs)
-        dc = lax.div(o, zs * xs)
-        x = lax.rem(my_x + dx, xs)
-        z = lax.rem(my_z + dz, zs)
-        return (x * zs + z) * cs + lax.rem(my_c + dc, cs)
-
+    across = []
+    for zz in range(zs):
+        dz = (zz + 1) // 2 if zz % 2 else zs - zz // 2
+        across.append(lax.rem(my_z + dz, zs) * cs)
+
+    def each_peer(visit):
+        def some(i, first):
+            dx, dc = lax.rem(i, xs), lax.div(i, xs)
+            base = lax.rem(my_x + dx, xs) * (zs * cs) + lax.rem(my_c + dc, cs)
+            for zz in range(first, zs):
+                visit(i * zs + zz, base + across[zz])
+            return 0
+
+        some(0, 1)
+        lax.fori_loop(1, xs * cs, lambda i, _: some(i, 0), 0)
+
+    smalls = [
+        pltpu.make_async_copy(src, dst, small.at[n])
+        for n, (src, dst) in enumerate(
+            (
+                (multi_in, multi),
+                (cheb_in, cheb),
+                (far_src_in, far_src),
+                (far_kind_in, far_kind),
+                (far_count_in, far_count),
+                (near_src_in, near_src),
+                (near_kind_in, near_kind),
+                (ghost_in, ghost),
+            )
+        )
+    ]
+    for copy in smalls:
+        copy.start()
     loads = [
         pltpu.make_async_copy(far_ops, ops_f, load.at[0]),
         pltpu.make_async_copy(near_ops, ops_n, load.at[1]),
         pltpu.make_async_copy(to_target, ops_t, load.at[2]),
     ]
+    barrier = pltpu.get_barrier_semaphore()
+    for d in (2, 1, 3):
+        pl.semaphore_signal(barrier, inc=1, device_id=helper(d), device_id_type=MESH)
+    each_peer(
+        lambda o, to: pl.semaphore_signal(barrier, inc=1, device_id=(to, h), device_id_type=MESH)
+    )
+
+    for copy in smalls:
+        copy.wait()
     for copy in loads:
         copy.start()
 
@@ -153,16 +201,6 @@
     live = pltpu.roll(near, 63, axis=1).astype(I32)
     iall[h, :, 384:512] = jnp.where(lane64 == 127, live, second(far_kind, 32))
 
-    barrier = pltpu.get_barrier_semaphore()
-    for d in range(1, 4):
-        pl.semaphore_signal(barrier, inc=1, device_id=helper(d), device_id_type=MESH)
-
-    def greet(o, _):
-        pl.semaphore_signal(barrier, inc=1, device_id=(peer(o), h), device_id_type=MESH)
-        return 0
-
-    lax.fori_loop(1, ranges, greet, 0)
-
     rows = ranges * 8
     step = min(128, rows)
     ghost_b = ghost[...].astype(F32).astype(BF)
@@ -170,9 +208,9 @@
     sub = iota((step, CAP), 0) % 8
     lane256 = iota((step, 256), 1)
     low_half = (iota((step, 256), 0) % 8) < 4
-
-    def build_pick(i, _):
-        at = pl.multiple_of(i * step, step)
+    fifth = (iota((step, 256), 0) % 8) == 4
+
+    def picker(at):
         own = ((iota((step, ranges), 0) + at) // 8) == iota((step, ranges), 1)
         each = dot(jnp.where(own, 1.0, 0.0).astype(BF), ghost_b)
 
@@ -183,16 +221,28 @@
         def put(ref, col, mask):
             ref[pl.ds(at, step), col : col + 256] = jnp.where(mask, 1.0, 0.0).astype(BF)
 
+        return chosen, put
+
+    def build_pick(i, _):
+        chosen, put = picker(pl.multiple_of(i * step, step))
         put(pick_f, 0, chosen(16 * h + sub))
         put(pick_f, 256, chosen(16 * h + 8 + sub))
+        return 0
+
+    lax.fori_loop(0, rows // step, build_pick, 0)
+
+    def build_late(i, _):
+        chosen, put = picker(pl.multiple_of(i * step, step))
         near = chosen(4 * h + sub % 4)
         put(pick_n, 0, near & low_half)
         put(pick_n, 256, near & jnp.logical_not(low_half))
         for t in range(4):
             put(pick_e, 256 * t, chosen(16 * h + 4 * t + sub % 4) & low_half)
-        return 0
-
-    lax.fori_loop(0, rows // step, build_pick, 0)
+            put(pick_e, 256 * (5 + t), chosen(4 * h + t) & fifth)
+        put(pick_e, 1024, near & low_half)
+        return 0
+
+    lax.fori_loop(0, rows // step, build_late, 0)
 
     for copy in loads:
         copy.wait()
@@ -238,9 +288,8 @@
         return copies
 
     y_copies = [to_helpers(0, mall), to_helpers(1, call), to_helpers(2, iall)]
-    for group in y_copies:
-        for copy in group:
-            copy.start()
+    for copy in y_copies[0] + y_copies[2][1:] + y_copies[1] + y_copies[2][:1]:
+        copy.start()
 
     lane = iota((BOX, 256), 1)
 
@@ -335,22 +384,19 @@
     def block(s, n):
         return pl.ds(pl.multiple_of(s * n, n), n)
 
-    def exchange(src, dst, s_sem, r_sem, o):
-        to = peer(o)
+    def exchange(src, dst, s_sem, r_sem, o, to):
+        n = src.shape[1]
+        take = 5 if n == 8 else n
         return pltpu.make_async_remote_copy(
-            src_ref=src.at[to],
-            dst_ref=dst.at[block(me, src.shape[1]), :],
+            src_ref=src.at[to, 0:take, :],
+            dst_ref=dst.at[pl.ds(pl.multiple_of(me * n, n), take), :],
             send_sem=s_sem.at[o],
             recv_sem=r_sem.at[o],
             device_id=(to, h),
             device_id_type=MESH,
         )
 
-    def send_far(o, _):
-        exchange(send_f, recv_f, f_send, f_recv, o).start()
-        return 0
-
-    lax.fori_loop(1, ranges, send_far, 0)
+    each_peer(lambda o, to: exchange(send_f, recv_f, f_send, f_recv, o, to).start())
     recv_f[block(me, 16), :] = send_f[me]
 
     own_cheb = jnp.concatenate([cheb[:, 0:512], rest], axis=1)
@@ -373,6 +419,16 @@
 
     put_tail(pl.ds(1024, BOX), tail)
 
+    def other_block(d):
+        g = lax.rem(h + d, 4)
+        keys(g)
+        count_block(g)
+
+    y_copies[2][1].wait()
+    other_block(3)
+    y_copies[2][2].wait()
+    other_block(1)
+
     for copy in y_copies[1]:
         copy.wait()
 
@@ -383,14 +439,30 @@
         hi, lo = split2(pltpu.roll(tails, TW * t, axis=1) if t else tails)
         w_pick[256 * (t + 1) : 256 * (t + 2), 0:128] = hi
         w_pick[256 * (t + 1) : 256 * (t + 2), 128:256] = lo
-    for l in range(5):
-        if l < 4:
-            part = call[:, :, 128 * l : 128 * l + 128].reshape(256, 128)
-        else:
-            part = jnp.where(lane_t < QW - 512, last, 0.0)
+    ends = jnp.where(lane_t < 32, last, 0.0)
+    blocks = [call[:, :, 128 * l : 128 * l + 128].reshape(256, 128) for l in range(4)]
+    blocks.append(pltpu.roll(ends, 96, axis=1))
+    ends = jnp.where((lane_t >= 32) & (lane_t < QW - 512), last, 0.0)
+    for c in range(4):
+        blocks.append(pltpu.roll(ends, (96 + 16 * c) % 128, axis=1) if c != 2 else ends)
+    for l, part in enumerate(blocks):
         hi, lo = split2(part)
         w_pick[256 * (l + 5) : 256 * (l + 6), 0:128] = hi
         w_pick[256 * (l + 5) : 256 * (l + 6), 128:256] = lo
+
+    def pick_ends(i, _):
+        at = pl.multiple_of(i * step, step)
+        both = dot(pick_e[pl.ds(at, step), 0:1024], w_pick[256:1280, :])
+        both = both + dot(pick_e[pl.ds(at, step), 1024:2304], w_pick[256 * 9 : 256 * 14, :])
+        send_e[pl.ds(i * messages, messages), :, :] = (both[:, :128] + both[:, 128:]).reshape(
+            messages, 8, 128
+        )
+        return 0
+
+    lax.fori_loop(0, rows // step, pick_ends, 0)
+
+    each_peer(lambda o, to: exchange(send_e, recv_e, e_send, e_recv, o, to).start())
+    recv_e[block(me, 8), :] = send_e[me]
 
     def pick_near(i, _):
         at = pl.multiple_of(i * step, step)
@@ -401,36 +473,17 @@
             send_n[to, 8 * half : 8 * half + 8, :] = (both[:, :128] + both[:, 128:]).reshape(
                 messages, 8, 128
             )
-        both = dot(pick_e[pl.ds(at, step), 0:1024], w_pick[256:1280, :])
-        both = both + dot(near[:, 256:], w_pick[256 * 9 : 256 * 10, :])
-        send_n[to, 16:24, :] = (both[:, :128] + both[:, 128:]).reshape(messages, 8, 128)
         return 0
 
     lax.fori_loop(0, rows // step, pick_near, 0)
 
-    def send_near(o, _):
-        exchange(send_n, recv_n, n_send, n_recv, o).start()
-        return 0
-
-    lax.fori_loop(1, ranges, send_near, 0)
-    recv_n[block(me, 24), :] = send_n[me]
-
-    for copy in y_copies[2]:
-        copy.wait()
-
-    def other_block(d, _):
-        g = lax.rem(h + d, 4)
-        keys(g)
-        count_block(g)
-        return 0
-
-    lax.fori_loop(1, 4, other_block, 0)
-
-    def far_arrived(o, _):
-        exchange(send_f, recv_f, f_send, f_recv, o).wait()
-        return 0
-
-    lax.fori_loop(1, ranges, far_arrived, 0)
+    each_peer(lambda o, to: exchange(send_n, recv_n, n_send, n_recv, o, to).start())
+    recv_n[block(me, 16), :] = send_n[me]
+
+    y_copies[2][0].wait()
+    other_block(2)
+
+    each_peer(lambda o, to: exchange(send_f, recv_f, f_send, f_recv, o, to).wait())
     for c in range(16):
         hi, lo = split2(recv_f[pl.ds(c, ranges, stride=16), :])
         w_main[64 * c : 64 * c + ranges, 0:128] = hi
@@ -446,26 +499,13 @@
 
     lax.fori_loop(0, 4096 // tall, far_rows, 0)
 
-    def near_arrived(o, _):
-        exchange(send_n, recv_n, n_send, n_recv, o).wait()
-        return 0
-
-    lax.fori_loop(1, ranges, near_arrived, 0)
+    each_peer(lambda o, to: exchange(send_e, recv_e, e_send, e_recv, o, to).wait())
     for q in range(4):
-        x = recv_n[pl.ds(16 + q, ranges, stride=24), :]
+        x = recv_e[pl.ds(q, ranges, stride=8), :]
         for t in range(4):
             moved = pltpu.roll(x, 128 - TW * t, axis=1) if t else x
             at = 256 * t + 64 * q
             put_tail(pl.ds(at, ranges), moved)
-    if ranges < 64:
-        w_near[...] = jnp.zeros_like(w_near)
-    for c in range(4):
-        for l in range(5):
-            row = 4 * l + c if l < 4 else 20 + c
-            x = recv_n[pl.ds(row, ranges, stride=24), :]
-            hi, lo = split2(x)
-            w_near[64 * c : 64 * c + ranges, 128 * l : 128 * l + 128] = hi
-            w_near[64 * c : 64 * c + ranges, QP + 128 * l : QP + 128 * l + 128] = lo
 
     def far_rows_tail(i, _):
         at = pl.ds(pl.multiple_of(i * tall, tall), tall)
@@ -474,14 +514,6 @@
         return 0
 
     lax.fori_loop(0, 4096 // tall, far_rows_tail, 0)
-
-    for k in range(NCLS):
-        m = jnp.concatenate(
-            [ncount[pl.ds(k, 256, stride=16), :], ncount[pl.ds(4 + k, 256, stride=16), :]], axis=1
-        ).astype(BF)
-        hi, lo = split2(near_sum[k] + dot(m, w_near[:, 0:QP]) + dot(m, w_near[:, QP:]))
-        parts[0:256, QP * k : QP * k + QP] = hi
-        parts[256:512, QP * k : QP * k + QP] = lo
 
     group = 4
     local_sum[...] = jnp.zeros_like(local_sum)
@@ -503,18 +535,55 @@
     lax.fori_loop(0, FCLS // group, far_class, 0)
 
     lh, ll = split2(local_sum[...])
-    local_parts = jnp.concatenate([lh, ll], axis=0)
+    left = jnp.concatenate([lh, ll, lh], axis=1)
+    total_far[...] = dot(left, jnp.concatenate([t_hi[...], t_hi[...], t_lo[...]], axis=0))
+
+    if ranges < 64:
+        w_near[...] = jnp.zeros_like(w_near)
+
+    def put_near(c, l, x):
+        hi, lo = split2(x)
+        w_near[64 * c : 64 * c + ranges, 128 * l : 128 * l + 128] = hi
+        w_near[64 * c : 64 * c + ranges, QP + 128 * l : QP + 128 * l + 128] = lo
+
+    fifths = recv_e[pl.ds(4, ranges, stride=8), :]
+    lane_r = iota((ranges, 128), 1)
+    for c in range(4):
+        first = pltpu.roll(recv_e[pl.ds(c, ranges, stride=8), :], 32, axis=1)
+        second = pltpu.roll(fifths, 32 - 16 * c, axis=1) if c < 2 else (
+            pltpu.roll(fifths, 128 + 32 - 16 * c, axis=1) if c > 2 else fifths
+        )
+        x = jnp.where(lane_r < 32, first, jnp.where(lane_r < QW - 512, second, 0.0))
+        put_near(c, 4, x)
+
+    each_peer(lambda o, to: exchange(send_n, recv_n, n_send, n_recv, o, to).wait())
+    for c in range(4):
+        for l in range(4):
+            put_near(c, l, recv_n[pl.ds(4 * l + c, ranges, stride=16), :])
+
+    for k in range(NCLS):
+        m = jnp.concatenate(
+            [ncount[pl.ds(k, 256, stride=16), :], ncount[pl.ds(4 + k, 256, stride=16), :]], axis=1
+        ).astype(BF)
+        hi, lo = split2(near_sum[k] + dot(m, w_near[:, 0:QP]) + dot(m, w_near[:, QP:]))
+        parts[0:256, QP * k : QP * k + QP] = hi
+        parts[256:512, QP * k : QP * k + QP] = lo
+
     back = []
-    for n, (n0, w) in enumerate(((0, 256), (256, 256), (512, 128))):
+    for n, (n0, w) in enumerate(((512, 128), (0, 256), (256, 256))):
         cols = slice(n0, n0 + w)
-        both = dot(parts[...], n_hi[:, cols]) + dot(local_parts, t_hi[:, cols])
-        total = both[0:256] + both[256:512]
-        total = total + dot(parts[0:256, :], n_lo[:, cols]) + dot(lh, t_lo[:, cols])
-        rs_send[:, :, cols] = total.reshape(4, BOX, w)
+        left = jnp.concatenate([parts[0:256, :], parts[256:512, :], parts[0:256, :]], axis=1)
+        right = jnp.concatenate([n_hi[:, cols], n_hi[:, cols], n_lo[:, cols]], axis=0)
+        total = (dot(left, right) + total_far[:, cols]).reshape(4, BOX, w)
+        if n == 0:
+            fold[...] = total[:, 0:32, :] + pltpu.roll(total[:, 32:64, :], 64, axis=2)
+        else:
+            rs_send[:, :, cols] = total
         for d in (2, 1, 3):
+            to = lax.rem(h + d, 4)
             copy = pltpu.make_async_remote_copy(
-                src_ref=rs_send.at[lax.rem(h + d, 4), :, cols],
-                dst_ref=rs_recv.at[d - 1, :, cols],
+                src_ref=rs_send.at[to, :, cols] if n else fold.at[to],
+                dst_ref=rs_recv.at[d - 1, :, cols] if n else fold_recv.at[d - 1],
                 send_sem=r_send.at[3 * n + d - 1],
                 recv_sem=r_recv.at[3 * n + d - 1],
                 device_id=helper(d),
@@ -524,8 +593,10 @@
             back.append(copy)
     for copy in back:
         copy.wait()
-    total = rs_send[h] + rs_recv[0] + rs_recv[1] + rs_recv[2]
-    out[...] = total[:, :QW]
+    out[:, 0:512] = rs_send[h] + rs_recv[0] + rs_recv[1] + rs_recv[2]
+    total = fold[h] + fold_recv[0] + fold_recv[1] + fold_recv[2]
+    out[0:32, 512:QW] = total[:, 0 : QW - 512]
+    out[32:64, 512:QW] = pltpu.roll(total, 64, axis=1)[:, 0 : QW - 512]
 
 
 def shards(sizes, multi, cheb, ghost, far_src, far_kind, far_count, near_src, near_kind, far_ops, near_ops, to_target):
@@ -537,21 +608,31 @@
     dma = pltpu.SemaphoreType.DMA
     return pl.pallas_call(
         functools.partial(evaluate, sizes),
-        out_shape=jax.ShapeDtypeStruct((BOX, QW), F32),
-        in_specs=[vmem] * 8 + [hbm] * 3,
+        out_shape=pltpu.VMEM((BOX, QW), F32),
+        in_specs=[hbm] * 11,
         out_specs=vmem,
         scratch_shapes=[
+            pltpu.VMEM((BOX, PW), F32),
+            pltpu.VMEM((BOX, QW), F32),
+            pltpu.VMEM((ranges, CAP), I32),
+            pltpu.VMEM((BOX, FAR), I32),
+            pltpu.VMEM((BOX, FAR), I32),
+            pltpu.VMEM((1, BOX), I32),
+            pltpu.VMEM((NEAR, BOX), I32),
+            pltpu.VMEM((NEAR, BOX), I32),
             pltpu.VMEM((4, BOX, 128), F32),
             pltpu.VMEM((4, BOX, QP), F32),
             pltpu.VMEM((4, BOX, 512), I32),
             pltpu.VMEM((ranges, 16, 128), F32),
-            pltpu.VMEM((ranges, 24, 128), F32),
+            pltpu.VMEM((ranges, 16, 128), F32),
+            pltpu.VMEM((ranges, 8, 128), F32),
             pltpu.VMEM((ranges * 16, 128), F32),
-            pltpu.VMEM((ranges * 24, 128), F32),
+            pltpu.VMEM((ranges * 16, 128), F32),
+            pltpu.VMEM((ranges * 8, 128), F32),
             pltpu.VMEM((rows, 512), BF),
             pltpu.VMEM((rows, 512), BF),
-            pltpu.VMEM((rows, 1024), BF),
-            pltpu.VMEM((2560, 256), BF),
+            pltpu.VMEM((rows, 2304), BF),
+            pltpu.VMEM((256 * 14, 256), BF),
             pltpu.VMEM((128, 128), F32),
             pltpu.VMEM((256, 256), F32),
             pltpu.VMEM((256, 256), F32),
@@ -573,11 +654,16 @@
             pltpu.VMEM((256, QP), BF),
             pltpu.VMEM((256, 256), F32),
             pltpu.VMEM((NCLS, 256, QP), F32),
+            pltpu.VMEM((256, QP), F32),
             pltpu.VMEM((512, NCLS * QP), BF),
-            pltpu.VMEM((4, BOX, QP), F32),
-            pltpu.VMEM((3, BOX, QP), F32),
+            pltpu.VMEM((4, BOX, 512), F32),
+            pltpu.VMEM((3, BOX, 512), F32),
+            pltpu.VMEM((4, 32, 128), F32),
+            pltpu.VMEM((3, 32, 128), F32),
             dma((9,)),
             dma((9,)),
+            dma((ranges,)),
+            dma((ranges,)),
             dma((ranges,)),
             dma((ranges,)),
             dma((ranges,)),
@@ -585,6 +671,7 @@
             dma((9,)),
             dma((9,)),
             dma((3,)),
+            dma((8,)),
         ],
         compiler_params=pltpu.CompilerParams(
             collective_id=0, has_side_effects=True, vmem_limit_bytes=60 * 1024 * 1024

time: 73.9 us -> 64 us (0.87)
  Pallas kernels: 72.2 us -> 63.2 us
  local copies, waits for them, and re-layouts: 1.59 us -> 0.67 us
    pallas_call x1, Pallas kernels: 72.2 us -> 63.2 us  [shards(): pl.pallas_call(functools.partial(evaluate, sizes), out_shape=pltpu.VMEM((...]
    unnamed x1, local copies, waits for them, and re-layouts: 1.59 us -> 0.67 us
where the time goes in v3:
time: 64 us; the launch traced here: 63.9 us
  Pallas kernels  63.2 us (99%)
  local copies, waits for them, and re-layouts  0.67 us (1%)
    pallas_call x1, Pallas kernels, shards(): pl.pallas_call(functools.partial(evaluate, sizes), out_shape=pltpu.VMEM((...  63.2 us

profile of v3, /device:TPU:1, one launch (start us, length us, event | category | flops | bytes accessed | tf_op | source)
XLA Modules:
  0.0 63.9 jit_solution(987509530735816321)
XLA Ops:
  0.0 63.2 %evaluate.1 = f32[64,560]{1,0:T(8,128)S(1)} custom-call(f32[64,152]{1,0:T(8,128)} %multi_in.1, f32[64,560]{1,0:T(8,128)} %cheb_in.1, s32[64,64]{1,0:T(8,128)} %ghost_in.1, s32[64,189]{1,0:T(8,128)} %far_src_in.1, s32[64,189]{1,0:T(8,128)} %far_kind_in.1, s32[1,64]{1,0:T(1,128)} %bitcast.5, s32[27,64]{1,0:T(8,128)} %bitcast.3, s32[27,64]{1,0:T(8,128)} %bitcast.4, ...), custom_call_target="tpu_custom_call" | custom-call | tf_op jit(solution)/shard_map/evaluate/pallas_call | solution.py:609
  63.2 0.7 %copy.13 = f32[64,560]{1,0:T(8,128)} copy(f32[64,560]{1,0:T(8,128)S(1)} %evaluate.1) | data formatting | bytes 286720

commit v4 on v3

--- a/solution.py
+++ b/solution.py
@@ -246,17 +246,8 @@
 
     for copy in loads:
         copy.wait()
-    for ref in (f_hi, f_lo, n_hi, n_lo, t_hi, t_lo, near_sum, w_main, w_tail):
-        ref[...] = jnp.zeros_like(ref)
-
-    def split_far_op(k, _):
-        hi, lo = split2(ops_f[k])
-        at = pl.ds(pl.multiple_of(k * 256, 256), PW)
-        f_hi[at, 0:PW] = hi
-        f_lo[at, 0:PW] = lo
-        return 0
-
-    lax.fori_loop(0, FCLS, split_far_op, 0)
+    n_hi[...] = jnp.zeros_like(n_hi)
+    n_lo[...] = jnp.zeros_like(n_lo)
 
     def split_near_op(k, _):
         hi, lo = split2(ops_n[k])
@@ -266,10 +257,6 @@
         return 0
 
     lax.fori_loop(0, NCLS, split_near_op, 0)
-    hi, lo = split2(ops_t[...])
-    t_hi[0:PW, 0:QW] = hi
-    t_lo[0:PW, 0:QW] = lo
-
     pl.semaphore_wait(barrier, ranges - 1 + 3)
 
     def to_helpers(k, ref):
@@ -290,6 +277,22 @@
     y_copies = [to_helpers(0, mall), to_helpers(1, call), to_helpers(2, iall)]
     for copy in y_copies[0] + y_copies[2][1:] + y_copies[1] + y_copies[2][:1]:
         copy.start()
+
+    for ref in (f_hi, f_lo, t_hi, t_lo, near_sum, w_main, w_tail):
+        ref[...] = jnp.zeros_like(ref)
+
+    def split_far_op(k, _):
+        hi, lo = split2(ops_f[k])
+        at = pl.ds(pl.multiple_of(k * 256, 256), PW)
+        f_hi[at, 0:PW] = hi
+        f_lo[at, 0:PW] = lo
+        return 0
+
+    lax.fori_loop(0, FCLS, split_far_op, 0)
+
+    hi, lo = split2(ops_t[...])
+    t_hi[0:PW, 0:QW] = hi
+    t_lo[0:PW, 0:QW] = lo
 
     lane = iota((BOX, 256), 1)
 
@@ -489,7 +492,7 @@
         w_main[64 * c : 64 * c + ranges, 0:128] = hi
         w_main[64 * c : 64 * c + ranges, 128:256] = lo
 
-    tall = 1024
+    tall = 2048
 
     def far_rows(i, _):
         at = pl.ds(pl.multiple_of(i * tall, tall), tall)
@@ -572,9 +575,13 @@
     back = []
     for n, (n0, w) in enumerate(((512, 128), (0, 256), (256, 256))):
         cols = slice(n0, n0 + w)
-        left = jnp.concatenate([parts[0:256, :], parts[256:512, :], parts[0:256, :]], axis=1)
         right = jnp.concatenate([n_hi[:, cols], n_hi[:, cols], n_lo[:, cols]], axis=0)
-        total = (dot(left, right) + total_far[:, cols]).reshape(4, BOX, w)
+        halves = []
+        for m in (0, 128):
+            high, low = parts[m : m + 128, :], parts[256 + m : 384 + m, :]
+            halves.append(dot(jnp.concatenate([high, low, high], axis=1), right))
+        total = jnp.concatenate(halves, axis=0)
+        total = (total + total_far[:, cols]).reshape(4, BOX, w)
         if n == 0:
             fold[...] = total[:, 0:32, :] + pltpu.roll(total[:, 32:64, :], 64, axis=2)
         else:

time: 64 us -> 64.6 us (level)
  no operation moved by 1% of the time
where the time goes in v4:
time: 64.6 us; the launch traced here: 64.5 us
  Pallas kernels  63.8 us (99%)
  local copies, waits for them, and re-layouts  0.67 us (1%)
    pallas_call x1, Pallas kernels, shards(): pl.pallas_call(functools.partial(evaluate, sizes), out_shape=pltpu.VMEM((...  63.8 us

profile of v4, /device:TPU:1, one launch (start us, length us, event | category | flops | bytes accessed | tf_op | source)
XLA Modules:
  0.0 64.5 jit_solution(683386202874477001)
XLA Ops:
  0.0 63.8 %evaluate.1 = f32[64,560]{1,0:T(8,128)S(1)} custom-call(f32[64,152]{1,0:T(8,128)} %multi_in.1, f32[64,560]{1,0:T(8,128)} %cheb_in.1, s32[64,64]{1,0:T(8,128)} %ghost_in.1, s32[64,189]{1,0:T(8,128)} %far_src_in.1, s32[64,189]{1,0:T(8,128)} %far_kind_in.1, s32[1,64]{1,0:T(1,128)} %bitcast.5, s32[27,64]{1,0:T(8,128)} %bitcast.3, s32[27,64]{1,0:T(8,128)} %bitcast.4, ...), custom_call_target="tpu_custom_call" | custom-call | tf_op jit(solution)/shard_map/evaluate/pallas_call | solution.py:616
  63.8 0.7 %copy.13 = f32[64,560]{1,0:T(8,128)} copy(f32[64,560]{1,0:T(8,128)S(1)} %evaluate.1) | data formatting | bytes 286720

commit v5 on v4

--- a/solution.py
+++ b/solution.py
@@ -16,6 +16,7 @@
 TW = PW - 128
 QW = 560
 QP = 640
+NW = 768
 FAR = 189
 NEAR = 27
 NEAR_AT = 192
@@ -492,7 +493,7 @@
         w_main[64 * c : 64 * c + ranges, 0:128] = hi
         w_main[64 * c : 64 * c + ranges, 128:256] = lo
 
-    tall = 2048
+    tall = 1024
 
     def far_rows(i, _):
         at = pl.ds(pl.multiple_of(i * tall, tall), tall)
@@ -539,7 +540,7 @@
 
     lh, ll = split2(local_sum[...])
     left = jnp.concatenate([lh, ll, lh], axis=1)
-    total_far[...] = dot(left, jnp.concatenate([t_hi[...], t_hi[...], t_lo[...]], axis=0))
+    total_far[:, 0:QP] = dot(left, jnp.concatenate([t_hi[...], t_hi[...], t_lo[...]], axis=0))
 
     if ranges < 64:
         w_near[...] = jnp.zeros_like(w_near)
@@ -572,35 +573,59 @@
         parts[0:256, QP * k : QP * k + QP] = hi
         parts[256:512, QP * k : QP * k + QP] = lo
 
-    back = []
-    for n, (n0, w) in enumerate(((512, 128), (0, 256), (256, 256))):
-        cols = slice(n0, n0 + w)
+    total_far[:, QP:NW] = jnp.zeros((256, NW - QP), F32)
+
+    def folded(d):
+        return pltpu.make_async_remote_copy(
+            src_ref=fold.at[lax.rem(h + d, 4)],
+            dst_ref=fold_recv.at[d - 1],
+            send_sem=r_send.at[d - 1],
+            recv_sem=r_recv.at[d - 1],
+            device_id=helper(d),
+            device_id_type=MESH,
+        )
+
+    def wide(n, d):
+        cols = pl.ds(pl.multiple_of((n - 1) * 256, 256), 256)
+        return pltpu.make_async_remote_copy(
+            src_ref=rs_send.at[lax.rem(h + d, 4), :, cols],
+            dst_ref=rs_recv.at[d - 1, :, cols],
+            send_sem=r_send.at[3 * n + d - 1],
+            recv_sem=r_recv.at[3 * n + d - 1],
+            device_id=helper(d),
+            device_id_type=MESH,
+        )
+
+    def give_back(n, _):
+        at = pl.multiple_of(lax.rem(n + 2, 3) * 256, 256)
+        cols = pl.ds(at, 256)
         right = jnp.concatenate([n_hi[:, cols], n_hi[:, cols], n_lo[:, cols]], axis=0)
         halves = []
         for m in (0, 128):
             high, low = parts[m : m + 128, :], parts[256 + m : 384 + m, :]
             halves.append(dot(jnp.concatenate([high, low, high], axis=1), right))
         total = jnp.concatenate(halves, axis=0)
-        total = (total + total_far[:, cols]).reshape(4, BOX, w)
-        if n == 0:
-            fold[...] = total[:, 0:32, :] + pltpu.roll(total[:, 32:64, :], 64, axis=2)
-        else:
-            rs_send[:, :, cols] = total
-        for d in (2, 1, 3):
-            to = lax.rem(h + d, 4)
-            copy = pltpu.make_async_remote_copy(
-                src_ref=rs_send.at[to, :, cols] if n else fold.at[to],
-                dst_ref=rs_recv.at[d - 1, :, cols] if n else fold_recv.at[d - 1],
-                send_sem=r_send.at[3 * n + d - 1],
-                recv_sem=r_recv.at[3 * n + d - 1],
-                device_id=helper(d),
-                device_id_type=MESH,
-            )
-            copy.start()
-            back.append(copy)
+        rs_send[:, :, cols] = (total + total_far[:, cols]).reshape(4, BOX, 256)
+
+        @pl.when(n == 0)
+        def _():
+            narrow = rs_send[:, :, 512:640]
+            fold[...] = narrow[:, 0:32, :] + pltpu.roll(narrow[:, 32:64, :], 64, axis=2)
+            for d in (2, 1, 3):
+                folded(d).start()
+
+        @pl.when(n > 0)
+        def _():
+            for d in (2, 1, 3):
+                wide(n, d).start()
+
+        return 0
+
+    lax.fori_loop(0, 3, give_back, 0)
+    back = [folded(d) for d in (2, 1, 3)] + [wide(n, d) for n in (1, 2) for d in (2, 1, 3)]
     for copy in back:
         copy.wait()
-    out[:, 0:512] = rs_send[h] + rs_recv[0] + rs_recv[1] + rs_recv[2]
+    out[:, 0:512] = rs_send[h, :, 0:512] + rs_recv[0] + rs_recv[1] + rs_recv[2]
     total = fold[h] + fold_recv[0] + fold_recv[1] + fold_recv[2]
     out[0:32, 512:QW] = total[:, 0 : QW - 512]
     out[32:64, 512:QW] = pltpu.roll(total, 64, axis=1)[:, 0 : QW - 512]
@@ -655,15 +680,15 @@
             pltpu.VMEM((PW, QW), F32),
             pltpu.VMEM((FCLS * 256, 256), BF),
             pltpu.VMEM((FCLS * 256, 256), BF),
-            pltpu.VMEM((NCLS * QP, QP), BF),
-            pltpu.VMEM((NCLS * QP, QP), BF),
+            pltpu.VMEM((NCLS * QP, NW), BF),
+            pltpu.VMEM((NCLS * QP, NW), BF),
             pltpu.VMEM((256, QP), BF),
             pltpu.VMEM((256, QP), BF),
             pltpu.VMEM((256, 256), F32),
             pltpu.VMEM((NCLS, 256, QP), F32),
-            pltpu.VMEM((256, QP), F32),
+            pltpu.VMEM((256, NW), F32),
             pltpu.VMEM((512, NCLS * QP), BF),
-            pltpu.VMEM((4, BOX, 512), F32),
+            pltpu.VMEM((4, BOX, NW), F32),
             pltpu.VMEM((3, BOX, 512), F32),
             pltpu.VMEM((4, 32, 128), F32),
             pltpu.VMEM((3, 32, 128), F32),

time: 64.6 us -> 63.7 us (0.986)
  Pallas kernels: 63.8 us -> 62.9 us
    pallas_call x1, Pallas kernels: 63.8 us -> 62.9 us  [shards(): pl.pallas_call(functools.partial(evaluate, sizes), out_shape=pltpu.VMEM((...]
where the time goes in v5:
time: 63.7 us; the launch traced here: 63.6 us
  Pallas kernels  62.9 us (99%)
  local copies, waits for them, and re-layouts  0.67 us (1%)
    pallas_call x1, Pallas kernels, shards(): pl.pallas_call(functools.partial(evaluate, sizes), out_shape=pltpu.VMEM((...  62.9 us

profile of v5, /device:TPU:1, one launch (start us, length us, event | category | flops | bytes accessed | tf_op | source)
XLA Modules:
  0.0 63.6 jit_solution(2704504317642301170)
XLA Ops:
  0.0 62.9 %evaluate.1 = f32[64,560]{1,0:T(8,128)S(1)} custom-call(f32[64,152]{1,0:T(8,128)} %multi_in.1, f32[64,560]{1,0:T(8,128)} %cheb_in.1, s32[64,64]{1,0:T(8,128)} %ghost_in.1, s32[64,189]{1,0:T(8,128)} %far_src_in.1, s32[64,189]{1,0:T(8,128)} %far_kind_in.1, s32[1,64]{1,0:T(1,128)} %bitcast.5, s32[27,64]{1,0:T(8,128)} %bitcast.3, s32[27,64]{1,0:T(8,128)} %bitcast.4, ...), custom_call_target="tpu_custom_call" | custom-call | tf_op jit(solution)/shard_map/evaluate/pallas_call | solution.py:641
  62.9 0.7 %copy.13 = f32[64,560]{1,0:T(8,128)} copy(f32[64,560]{1,0:T(8,128)S(1)} %evaluate.1) | data formatting | bytes 286720

commit v6 on v5

--- a/solution.py
+++ b/solution.py
@@ -137,12 +137,12 @@
         def some(i, first):
             dx, dc = lax.rem(i, xs), lax.div(i, xs)
             base = lax.rem(my_x + dx, xs) * (zs * cs) + lax.rem(my_c + dc, cs)
-            for zz in range(first, zs):
+            for zz in reversed(range(first, zs)):
                 visit(i * zs + zz, base + across[zz])
             return 0
 
+        lax.fori_loop(1, xs * cs, lambda i, _: some(xs * cs - i, 0), 0)
         some(0, 1)
-        lax.fori_loop(1, xs * cs, lambda i, _: some(i, 0), 0)
 
     smalls = [
         pltpu.make_async_copy(src, dst, small.at[n])

time: 63.7 us -> 60.8 us (0.954)
  the two profiles are of different devices: /device:TPU:1 before, /device:TPU:2 now
where the time goes in v6:
time: 60.8 us; the launch traced here: 60.7 us
  Pallas kernels  60 us (99%)
  local copies, waits for them, and re-layouts  0.67 us (1%)
    pallas_call x1, Pallas kernels, shards(): pl.pallas_call(functools.partial(evaluate, sizes), out_shape=pltpu.VMEM((...  60 us

profile of v6, /device:TPU:2, one launch (start us, length us, event | category | flops | bytes accessed | tf_op | source)
XLA Modules:
  0.0 60.7 jit_solution(9932123627736975538)
XLA Ops:
  0.0 60.0 %evaluate.1 = f32[64,560]{1,0:T(8,128)S(1)} custom-call(f32[64,152]{1,0:T(8,128)} %multi_in.1, f32[64,560]{1,0:T(8,128)} %cheb_in.1, s32[64,64]{1,0:T(8,128)} %ghost_in.1, s32[64,189]{1,0:T(8,128)} %far_src_in.1, s32[64,189]{1,0:T(8,128)} %far_kind_in.1, s32[1,64]{1,0:T(1,128)} %bitcast.5, s32[27,64]{1,0:T(8,128)} %bitcast.3, s32[27,64]{1,0:T(8,128)} %bitcast.4, ...), custom_call_target="tpu_custom_call" | custom-call | tf_op jit(solution)/shard_map/evaluate/pallas_call | solution.py:641
  60.0 0.7 %copy.13 = f32[64,560]{1,0:T(8,128)} copy(f32[64,560]{1,0:T(8,128)S(1)} %evaluate.1) | data formatting | bytes 286720
